TPU v7x, 256 devices: a whole 4x4x8 slice. The times are simulated.
256 devices in a mesh: dp: 32 (over y_hi, z, core), tp: 8 (over x, y_lo).
Axes of the slice: x: 4, y: 4 (y_hi: 2, y_lo: 2; y = y_hi * 2 + y_lo), z: 8, core: 2. Of those that a mesh axis runs over, the one named last changes fastest.
Arguments:
- hidden: bfloat16 [32768, 4096], P(('dp', 'tp')), may hold values from -24 to 24
- query_grad: bfloat16 [32768, 4096], P('dp', 'tp'), may hold values from -1.5 to 1.5
- key_grad: bfloat16 [32768, 1024], P('dp', 'tp'), may hold values from -1.5 to 1.5
- value_grad: bfloat16 [32768, 1024], P('dp', 'tp'), may hold values from -1.5 to 1.5
- w_query: bfloat16 [4096, 4096], P(None, 'tp'), may hold values from -0.09375 to 0.09375
- w_key: bfloat16 [4096, 1024], P(None, 'tp'), may hold values from -0.09375 to 0.09375
- w_value: bfloat16 [4096, 1024], P(None, 'tp'), may hold values from -0.09375 to 0.09375
Outputs:
- hidden_grad: bfloat16 [32768, 4096], P(('dp', 'tp'))
- grad_query: float32 [4096, 4096], P('dp', 'tp')
- grad_key: float32 [4096, 1024], P('dp', 'tp')
- grad_value: float32 [4096, 1024], P('dp', 'tp')
All inputs are finite; a program needn't handle non-finite values.
Results may differ from a plain program's by a relative error of at most 0.014.
Values may be sent and summed in bfloat16 or wider, within the bound.
A program may use at most 256 MiB of HBM per device.

v0:
```python
import jax
import jax.numpy as jnp
from jax import lax
from jax.sharding import Mesh
from jax.sharding import PartitionSpec as P

TP = ("tp_0", "tp_1")
DP_TP = ("dp", "tp_0", "tp_1")


def scatter_axes(array, axes, dim):
    if not axes:
        return array
    nearer = lax.psum_scatter(array, axes[0], scatter_dimension=dim, tiled=True)
    return scatter_axes(nearer, axes[1:], dim)


def contract_rows(left, right):
    return lax.dot_general(
        left, right, (((0,), (0,)), ((), ())), preferred_element_type=jnp.float32
    )


def contract_cols(left, right):
    return lax.dot_general(
        left, right, (((1,), (1,)), ((), ())), preferred_element_type=jnp.float32
    )


def local(hidden, query_grad, key_grad, value_grad, w_query, w_key, w_value):
    query_width = w_query.shape[1]
    head_width = w_key.shape[1]
    all_grads = jnp.concatenate((query_grad, key_grad, value_grad), axis=1)
    all_weights = jnp.concatenate((w_query, w_key, w_value), axis=1)
    picked = all_grads
    total = contract_rows(lax.all_gather(hidden, TP, axis=0, tiled=True), picked)
    picked = all_grads
    summed = scatter_axes(contract_cols(picked, all_weights).astype(jnp.bfloat16), TP, 0).astype(
        jnp.float32
    )
    hidden_grad = summed.astype(jnp.bfloat16)
    weight_grad = lax.psum_scatter(
        total.astype(jnp.bfloat16), "dp", scatter_dimension=0, tiled=True
    ).astype(jnp.float32)
    grad_query = weight_grad[:, :query_width]
    grad_key = weight_grad[:, query_width : query_width + head_width]
    grad_value = weight_grad[:, query_width + head_width :]
    return (hidden_grad, grad_query, grad_key, grad_value)


def solution(mesh):
    torus = Mesh(mesh.devices.reshape(mesh.shape["dp"], 4, 2), ("dp", "tp_0", "tp_1"))
    in_specs = (
        P(DP_TP, None),
        P("dp", TP),
        P("dp", TP),
        P("dp", TP),
        P(None, TP),
        P(None, TP),
        P(None, TP),
    )
    out_specs = (P(DP_TP, None), P("dp", TP), P("dp", TP), P("dp", TP))
    return jax.shard_map(local, mesh=torus, in_specs=in_specs, out_specs=out_specs, check_vma=False)
```

profile of v0, /device:TPU:9, one launch (start us, length us, event | category | flops | bytes accessed | tf_op | source)
XLA Modules:
  0.0 387.0 jit_solution(8804540133229758166)
XLA Ops:
  8.0 0.0 all-gather.2.cloned.1.call-start
  8.0 0.7 all-gather.2.cloned.1.call-update
  8.7 0.0 reduce-scatter.6.cloned.1.call-start
  8.8 1.3 constant_dynamic-update-slice_fusion.2
  10.1 1.0 constant_dynamic-update-slice_fusion.1
  11.1 1.0 constant_dynamic-update-slice_fusion
  12.1 11.8 %convolution_convert_fusion = bf16[1024,4096]{1,0:T(8,128)(2,1)} fusion(bf16[1024,768]{1,0:T(8,128)(2,1)S(1)} %constant_dynamic-update-slice_fusion, bf16[4096,128]{1,0:T(8,128)(2,1)} %param.13, bf16[4096,128]{1,0:T(8,128)(2,1)} %param.12, bf16[4096,512]{1,0:T(8,128)(2,1)} %param.11), kind=kOutput, calls=%fused_computation | convolution fusion | flops 6465519616 | bytes 16252928 | tf_op jit(solution)/shard_map/dot_general | solution.py:25
  23.9 0.0 reduce-scatter.6.cloned.1.call-update
  23.9 0.0 reduce-scatter.10.cloned.1.call-start
  23.9 158.6 %all-gather.2.cloned.1.call-done = bf16[1024,4096]{1,0:T(8,128)(2,1)} async-done(((bf16[128,4096]{1,0:T(8,128)(2,1)}), bf16[1024,4096]{1,0:T(8,128)(2,1)}) %all-gather.2.cloned.1.call-update) | async-done | bytes 8388624 | tf_op jit(solution)/shard_map/all_gather | solution.py:36
  182.5 12.1 %fusion.5 = bf16[4096,768]{0,1:T(8,128)(2,1)} fusion(bf16[1024,768]{1,0:T(8,128)(2,1)S(1)} %constant_dynamic-update-slice_fusion, bf16[1024,4096]{1,0:T(8,128)(2,1)} %all-gather.2.cloned.1.call-done), kind=kOutput, calls=%fused_computation.7 | convolution fusion | flops 6445596672 | bytes 16252928 | tf_op jit(solution)/shard_map/dot_general | solution.py:19
  194.6 8.6 %copy.17 = bf16[4096,768]{1,0:T(8,128)(2,1)} copy(bf16[4096,768]{0,1:T(8,128)(2,1)} %fusion.5) | data formatting | bytes 12582912
  203.2 0.0 reduce-scatter.10.cloned.1.call-update
  203.2 0.0 reduce-scatter.8.cloned.1.call-start
  203.2 0.0 reduce-scatter.6.cloned.1.call-done
  203.3 0.5 reduce-scatter.8.cloned.1.call-update
  203.8 134.3 %reduce-scatter.10.cloned.1.call-done = bf16[128,768]{1,0:T(8,128)(2,1)} async-done(((bf16[4096,768]{1,0:T(8,128)(2,1)}), bf16[128,768]{1,0:T(8,128)(2,1)}) %reduce-scatter.10.cloned.1.call-update) | async-done | bytes 196624
  338.1 1.1 copy.18
  339.2 0.7 copy.16
  340.0 0.7 copy.15
  340.7 0.8 copy.14
  341.5 37.9 %reduce-scatter.8.cloned.1.call-done = bf16[128,4096]{1,0:T(8,128)(2,1)} async-done(((bf16[256,4096]{1,0:T(8,128)(2,1)}), bf16[128,4096]{1,0:T(8,128)(2,1)}) %reduce-scatter.8.cloned.1.call-update) | async-done | bytes 1048592 | tf_op jit(solution)/shard_map/reduce_scatter | solution.py:14
  (2 shorter events, 0.0 us)
Async XLA Ops:
  8.0 174.5 %all-gather.2.cloned.1.call-start = ((), (), s32[]{:S(2)}) async-start(), calls=%async_computation.5 | async-start | bytes 9437184 | tf_op jit(solution)/shard_map/all_gather | solution.py:36
  8.7 194.5 %reduce-scatter.6.cloned.1.call-start = ((), (), s32[]{:S(2)}) async-start(), calls=%async_computation.3 | async-start | bytes 10485760 | tf_op jit(solution)/shard_map/reduce_scatter | solution.py:14
  23.9 314.2 %reduce-scatter.10.cloned.1.call-start = ((), (), s32[]{:S(2)}) async-start(), calls=%async_computation.6 | async-start | bytes 6488064
  203.2 176.2 %reduce-scatter.8.cloned.1.call-start = ((), (), s32[]{:S(2)}) async-start(), calls=%async_computation.4 | async-start | bytes 3145728 | tf_op jit(solution)/shard_map/reduce_scatter | solution.py:14
Sparse Core Ops, SparseCore 0:
  10.6 171.9 all-gather.1
Sparse Core Ops, SparseCore 1:
  24.0 144.8 reduce-scatter.5
  203.3 134.8 reduce-scatter.9
  341.1 38.3 reduce-scatter.7
where the time goes:
time: 390 us; the launch traced here: 387 us
  waiting for transfers between devices  332 us (85%)
  matrix products  23.8 us (6%)
  between operations  15.7 us (4%)
  local copies, waits for them, and re-layouts  15.3 us (4%)
    all_gather x1, waiting for transfers between devices, local(): lax.all_gather(hidden, TP, axis=0, tiled=True)  159 us
    unnamed x5, waiting for transfers between devices  136 us
    reduce_scatter x2, waiting for transfers between devices, scatter_axes(): nearer = lax.psum_scatter(array, axes[0], scatter_dimension=dim, tiled=True)  37.9 us
    unnamed x7, local copies, waits for them, and re-layouts  14.3 us
    dot_general x1, matrix products, contract_rows(): lax.dot_general(left, right, (((0,), (0,)), ((), ())), preferred_element_...  12.1 us
    dot_general x1, matrix products, contract_cols(): lax.dot_general(left, right, (((1,), (1,)), ((), ())), preferred_element_...  11.8 us
  transfers between devices with their start and end apart: 4, of which 3 were waited for; matrix products, arithmetic and copies ran while one was open for 10% of the time, Pallas kernels for 0%

commit v1 on v0

v1 whole, which is shorter than its diff:
```python
import jax
import jax.numpy as jnp
from jax import lax
from jax.experimental import pallas as pl
from jax.experimental.pallas import tpu as pltpu
from jax.sharding import PartitionSpec as P

MESH = pl.DeviceIdType.MESH
BF16 = jnp.bfloat16
F32 = jnp.float32
T = 128
D = 4096
H = 2048
HH = 1024
CQ = 512
CK = 128
C = 768


def nt(left, right):
    return lax.dot_general(left, right, (((1,), (1,)), ((), ())), preferred_element_type=F32)


def tn(left, right):
    return lax.dot_general(left, right, (((0,), (0,)), ((), ())), preferred_element_type=F32)


def kernel(
    hidden_ref,
    q_ref,
    k_ref,
    v_ref,
    wq_ref,
    wk_ref,
    wv_ref,
    out_ref,
    gq_ref,
    gk_ref,
    gv_ref,
    hid,
    hsend,
    gown,
    goth,
    wmine,
    woth,
    wsend,
    hg,
    wg,
    ccs,
    ccr,
    xs,
    xr,
    zs,
    zr,
    fin,
    yr,
    yos,
    yor,
    lsem,
    ssem,
    rsem,
    yssem,
    yrsem,
):
    dp = lax.axis_index("dp")
    tp = lax.axis_index("tp")
    c = lax.rem(dp, 2)
    z = lax.rem(dp // 2, 8)
    yh = dp // 16
    yl = lax.rem(tp, 2)
    x = tp // 2
    e = lax.rem(z, 2)

    def dev(xx=None, yhh=None, yll=None, zz=None, cc=None):
        xx = x if xx is None else xx
        yhh = yh if yhh is None else yhh
        yll = yl if yll is None else yll
        zz = z if zz is None else zz
        cc = c if cc is None else cc
        return (yhh * 16 + zz * 2 + cc, xx * 2 + yll)

    XP = dev(xx=lax.rem(x + 1, 4))
    XM = dev(xx=lax.rem(x + 3, 4))
    YI = dev(yll=1 - yl)
    YO = dev(yhh=1 - yh, yll=1 - yl)
    Y2 = dev(yhh=1 - yh)
    ZP = dev(zz=lax.rem(z + 1, 8))
    ZM = dev(zz=lax.rem(z + 7, 8))
    ZX = dev(zz=z + 1 - 2 * e)
    CC = dev(cc=1 - c)

    counter = [0]
    sent = []

    def remote(src, dst, target, send=None, recv=None):
        if send is None:
            i = counter[0]
            counter[0] += 1
            send, recv = ssem.at[i], rsem.at[i]
        copy = pltpu.make_async_remote_copy(
            src_ref=src, dst_ref=dst, send_sem=send, recv_sem=recv, device_id=target, device_id_type=MESH
        )
        return copy

    def start(copy):
        copy.start()
        sent.append(copy)

    def local(src, dst, i):
        copy = pltpu.make_async_copy(src, dst, lsem.at[i])
        copy.start()
        return copy

    mine = pl.ds(pl.multiple_of(yl * H, H), H)
    other = pl.ds(pl.multiple_of((1 - yl) * H, H), H)
    load_a = local(hidden_ref.at[:, mine], hid.at[pl.ds(0, T)], 0)
    load_b = local(hidden_ref.at[:, other], hsend, 1)
    wrow = c * 1024 + e * 512
    wrows = pl.ds(pl.multiple_of((1 - yl) * H + wrow, 512), 512)
    local(wq_ref.at[wrows], wsend.at[:, pl.ds(0, CQ)], 2)
    local(wk_ref.at[wrows], wsend.at[:, pl.ds(CQ, CK)], 2)
    local(wv_ref.at[wrows], wsend.at[:, pl.ds(CQ + CK, CK)], 2)
    for r, off in enumerate((0, 1, 3, 2)):
        for s in range(2):
            block = lax.rem(x + off, 4) * 2 + (yl if s == 0 else 1 - yl)
            src = pl.ds(pl.multiple_of(block * T, T), T)
            dst = pl.ds(r * 256 + s * T, T)
            local(q_ref.at[src], gown.at[dst, pl.ds(0, CQ)], 3)
            local(k_ref.at[src], gown.at[dst, pl.ds(CQ, CK)], 3)
            local(v_ref.at[src], gown.at[dst, pl.ds(CQ + CK, CK)], 3)
    local(wq_ref.at[mine], wmine.at[:, pl.ds(0, CQ)], 4)
    local(wk_ref.at[mine], wmine.at[:, pl.ds(CQ, CK)], 4)
    local(wv_ref.at[mine], wmine.at[:, pl.ds(CQ + CK, CK)], 4)

    def wait_local(buffer, i):
        pltpu.make_async_copy(buffer, buffer, lsem.at[i]).wait()

    barrier = pltpu.get_barrier_semaphore()
    for target in (XP, XM, YI, YO, Y2, ZP, ZM, CC):
        pl.semaphore_signal(barrier, inc=1, device_id=target, device_id_type=MESH)
    pl.semaphore_wait(barrier, 8)

    def rows(r, s, half=None):
        first = r * 256 + s * T
        return pl.ds(first, T) if half is None else pl.ds(first + half * 64, 64)

    a_p = [remote(hid.at[rows(0, 0, i)], hid.at[rows(2, 0, i)], XP) for i in range(2)]
    a_m = [remote(hid.at[rows(0, 0, i)], hid.at[rows(1, 0, i)], XM) for i in range(2)]
    b_y = [remote(hsend.at[pl.ds(64 * i, 64)], hid.at[rows(0, 1, i)], YI) for i in range(2)]
    b_p = [remote(hid.at[rows(0, 1, i)], hid.at[rows(2, 1, i)], XP) for i in range(2)]
    b_m = [remote(hid.at[rows(0, 1, i)], hid.at[rows(1, 1, i)], XM) for i in range(2)]
    f_p = [remote(hid.at[rows(2, s, 0)], hid.at[rows(3, s, 0)], XP) for s in range(2)]
    f_m = [remote(hid.at[rows(1, s, 1)], hid.at[rows(3, s, 1)], XM) for s in range(2)]
    g_y = {
        (r, s): remote(gown.at[rows(r, s)], goth.at[rows(r, 1 - s)], YI) for r in (3, 1, 2, 0) for s in range(2)
    }

    def wpiece(cc, ee, k):
        return pl.ds(pl.multiple_of(cc * 1024 + ee * 512 + k * 256, 256), 256)

    w_y = [remote(wsend.at[pl.ds(256 * k, 256)], woth.at[wpiece(c, e, k)], YO) for k in range(2)]
    w_z = [remote(woth.at[wpiece(c, e, k)], woth.at[wpiece(c, e, k)], ZX) for k in range(2)]
    w_c = [remote(woth.at[wpiece(c, e, k)], woth.at[wpiece(c, e, k)], CC) for k in range(2)]
    w_d = [remote(woth.at[wpiece(c, 1 - e, k)], woth.at[wpiece(c, 1 - e, k)], CC) for k in range(2)]
    xc = {
        (d, b, s): remote(xs.at[d, b, s], xr.at[d, b, s], XP if d == 0 else XM)
        for d in range(2)
        for b in range(3)
        for s in range(2)
    }
    o_y = remote(yos, yor, YI)
    cc_copy = [remote(ccs.at[n], ccr.at[n], CC) for n in range(2)]
    steps = (pl.ds(0, 64), pl.ds(64, 128), pl.ds(192, 128), pl.ds(320, 128))
    zc = {
        (n, d, i): remote(zs.at[n, d, steps[i]], zr.at[n, d, steps[i]], ZP if d == 0 else ZM)
        for n in range(2)
        for d in range(2)
        for i in range(4)
    }

    load_a.wait()
    for i in range(2):
        start(a_p[i])
        start(a_m[1 - i])
    load_b.wait()
    for i in range(2):
        start(b_y[i])
    wait_local(wsend, 2)
    for k in range(2):
        start(w_y[k])
    wait_local(gown, 3)
    for r in (3, 1, 2, 0):
        for s in (0, 1):
            start(g_y[r, s])
    wait_local(wmine, 4)

    def hg_own():
        def step(n, carry):
            cols = pl.ds(pl.multiple_of(n * 256, 256), 256)
            w = wmine[cols, :]
            for m in range(2):
                hg[pl.ds(m * 512, 512), cols] = nt(gown[pl.ds(m * 512, 512), :], w)
            return carry

        lax.fori_loop(0, 8, step, 0)

    def hg_other(r):
        def step(n, carry):
            cols = pl.ds(pl.multiple_of(n * 256, 256), 256)
            hg[pl.ds(r * 256, 256), cols] += nt(goth[pl.ds(r * 256, 256), :], woth[cols, :])
            return carry

        lax.fori_loop(0, 8, step, 0)

    def wg_add(n, g, first, depth, fresh):
        def step(m, carry):
            cols = pl.ds(pl.multiple_of(m * 512, 512), 512)
            part = tn(hid[pl.ds(first, depth), cols], g[pl.ds(first, depth), :])
            if fresh:
                wg[n, cols, :] = part
            else:
                wg[n, cols, :] += part
            return carry

        lax.fori_loop(0, 4, step, 0)

    def cc_send(n):
        def step(zz, carry):
            src = pl.ds(pl.multiple_of((2 * zz + 1 - c) * T, T), T)
            dst = pl.ds(pl.multiple_of(zz * T, T), T)
            ccs[n, dst, :] = wg[n, src, :].astype(BF16)
            return carry

        lax.fori_loop(0, 8, step, 0)
        start(cc_copy[n])

    def pair_sum(n, zz, first=0, size=T):
        src = pl.ds(pl.multiple_of((2 * zz + c) * T + first, size), size)
        dst = pl.ds(pl.multiple_of(zz * T + first, size), size)
        return wg[n, src, :] + ccr[n, dst, :].astype(F32)

    def z_step(n, i):
        if i == 0:
            far = lax.rem(z + 4, 8)
            zs[n, 0, steps[0], :] = pair_sum(n, far, 0, 64).astype(BF16)
            zs[n, 1, steps[0], :] = pair_sum(n, far, 64, 64).astype(BF16)
        else:
            for d in range(2):
                zz = lax.rem(z + 4 - i, 8) if d == 0 else lax.rem(z + 4 + i, 8)
                zc[n, d, i - 1].wait_recv()
                if i == 1:
                    for half in range(2):
                        part = pair_sum(n, zz, half * 64, 64)
                        if half == d:
                            part = part + zr[n, d, steps[0], :].astype(F32)
                        zs[n, d, pl.ds(64 + half * 64, 64), :] = part.astype(BF16)
                else:
                    part = pair_sum(n, zz) + zr[n, d, steps[i - 1], :].astype(F32)
                    zs[n, d, steps[i], :] = part.astype(BF16)
                start(zc[n, d, i])
        if i == 0:
            for d in range(2):
                start(zc[n, d, 0])

    def z_last(n):
        for d in range(2):
            zc[n, d, 3].wait_recv()
        total = pair_sum(n, z) + zr[n, 0, steps[3], :].astype(F32) + zr[n, 1, steps[3], :].astype(F32)
        fin[n] = total.astype(BF16)

    left, right = pl.ds(0, HH), pl.ds(HH, HH)

    def x_far():
        for s in (1, 0):
            block = pl.ds(3 * 256 + s * T, T)
            xs[0, 0, s] = hg[block, left].astype(BF16)
            start(xc[0, 0, s])
            xs[1, 0, s] = hg[block, right].astype(BF16)
            start(xc[1, 0, s])

    def x_direct(s):
        xs[0, 1, s] = hg[pl.ds(1 * 256 + s * T, T), right].astype(BF16)
        start(xc[0, 1, s])
        xs[1, 1, s] = hg[pl.ds(2 * 256 + s * T, T), left].astype(BF16)
        start(xc[1, 1, s])

    def x_summed(s):
        xc[0, 0, s].wait_recv()
        xs[0, 2, s] = (hg[pl.ds(1 * 256 + s * T, T), left] + xr[0, 0, s].astype(F32)).astype(BF16)
        start(xc[0, 2, s])
        xc[1, 0, s].wait_recv()
        xs[1, 2, s] = (hg[pl.ds(2 * 256 + s * T, T), right] + xr[1, 0, s].astype(F32)).astype(BF16)
        start(xc[1, 2, s])

    def x_total(s):
        for d in range(2):
            xc[d, 1, s].wait_recv()
            xc[d, 2, s].wait_recv()
        block = pl.ds(s * T, T)
        lo = hg[block, left] + xr[0, 2, s].astype(F32) + xr[1, 1, s].astype(F32)
        hi = hg[block, right] + xr[0, 1, s].astype(F32) + xr[1, 2, s].astype(F32)
        return lo.astype(BF16), hi.astype(BF16)

    hg_own()
    a_p[0].wait_recv()
    start(f_p[0])
    a_m[1].wait_recv()
    start(f_m[0])
    w_y[0].wait_recv()
    start(w_z[0])
    start(w_c[0])
    for i in range(2):
        b_y[i].wait_recv()
    for i in range(2):
        start(b_p[i])
        start(b_m[1 - i])
    w_y[1].wait_recv()
    start(w_z[1])
    start(w_c[1])
    w_z[0].wait_recv()
    start(w_d[0])
    b_p[0].wait_recv()
    start(f_p[1])
    b_m[1].wait_recv()
    start(f_m[1])
    w_z[1].wait_recv()
    start(w_d[1])
    a_p[1].wait_recv()
    a_m[0].wait_recv()
    b_p[1].wait_recv()
    b_m[0].wait_recv()
    wg_add(0, gown, 0, 768, True)
    for k in range(2):
        w_c[k].wait_recv()
        w_d[k].wait_recv()
    g_y[3, 0].wait_recv()
    g_y[3, 1].wait_recv()
    hg_other(3)
    x_far()
    for s in range(2):
        f_p[s].wait_recv()
        f_m[s].wait_recv()
    wg_add(0, gown, 768, 256, False)
    cc_send(0)
    for r in (1, 2):
        g_y[r, 0].wait_recv()
        g_y[r, 1].wait_recv()
        hg_other(r)
    x_direct(1)
    cc_copy[0].wait_recv()
    z_step(0, 0)
    x_summed(1)
    x_direct(0)
    z_step(0, 1)
    g_y[0, 0].wait_recv()
    g_y[0, 1].wait_recv()
    wg_add(1, goth, 0, 1024, True)
    cc_send(1)
    x_summed(0)
    hg_other(0)
    cc_copy[1].wait_recv()
    z_step(1, 0)
    z_step(0, 2)
    z_step(1, 1)
    lo, hi = x_total(1)
    yos[:, left] = lo
    yos[:, right] = hi
    start(o_y)
    z_step(0, 3)
    z_step(1, 2)
    z_last(0)

    own_copy = remote(fin.at[0], yr.at[yh], dev(yhh=yl), yssem.at[0], yrsem.at[yh])
    other_copy = remote(fin.at[1], yr.at[yh], dev(yhh=yl, yll=1 - yl), yssem.at[1], yrsem.at[yh])

    @pl.when(yh != yl)
    def _():
        own_copy.start()

    z_step(1, 3)
    lo, hi = x_total(0)
    out_ref[:, pl.ds(pl.multiple_of(yl * H, H), HH)] = lo
    out_ref[:, pl.ds(pl.multiple_of(yl * H + HH, HH), HH)] = hi
    o_y.wait_recv()
    out_ref[:, pl.ds(pl.multiple_of((1 - yl) * H, H), H)] = yor[...]
    z_last(1)
    other_copy.start()

    def finish(total):
        gq_ref[...] = total[:, :CQ]
        gk_ref[...] = total[:, CQ : CQ + CK]
        gv_ref[...] = total[:, CQ + CK :]

    def arrived(slot):
        pltpu.make_async_copy(yr.at[slot], yr.at[slot], yrsem.at[slot]).wait()

    @pl.when(yh == yl)
    def _():
        arrived(1 - yh)
        finish(fin[0].astype(F32) + yr[1 - yh].astype(F32))

    @pl.when(yh != yl)
    def _():
        arrived(0)
        arrived(1)
        finish(yr[0].astype(F32) + yr[1].astype(F32))
        own_copy.wait_send()

    other_copy.wait_send()
    for copy in sent:
        copy.wait_send()


N_SEM = 80


def local_step(*args):
    vmem = pl.BlockSpec(memory_space=pltpu.VMEM)
    scratch = [
        pltpu.VMEM((1024, H), BF16),
        pltpu.VMEM((T, H), BF16),
        pltpu.VMEM((1024, C), BF16),
        pltpu.VMEM((1024, C), BF16),
        pltpu.VMEM((H, C), BF16),
        pltpu.VMEM((H, C), BF16),
        pltpu.VMEM((512, C), BF16),
        pltpu.VMEM((1024, H), F32),
        pltpu.VMEM((2, H, C), F32),
        pltpu.VMEM((2, 1024, C), BF16),
        pltpu.VMEM((2, 1024, C), BF16),
        pltpu.VMEM((2, 3, 2, T, HH), BF16),
        pltpu.VMEM((2, 3, 2, T, HH), BF16),
        pltpu.VMEM((2, 2, 448, C), BF16),
        pltpu.VMEM((2, 2, 448, C), BF16),
        pltpu.VMEM((2, T, C), BF16),
        pltpu.VMEM((2, T, C), BF16),
        pltpu.VMEM((T, H), BF16),
        pltpu.VMEM((T, H), BF16),
        pltpu.SemaphoreType.DMA((5,)),
        pltpu.SemaphoreType.DMA((N_SEM,)),
        pltpu.SemaphoreType.DMA((N_SEM,)),
        pltpu.SemaphoreType.DMA((2,)),
        pltpu.SemaphoreType.DMA((2,)),
    ]
    return pl.pallas_call(
        kernel,
        out_shape=(
            jax.ShapeDtypeStruct((T, D), BF16),
            jax.ShapeDtypeStruct((T, CQ), F32),
            jax.ShapeDtypeStruct((T, CK), F32),
            jax.ShapeDtypeStruct((T, CK), F32),
        ),
        in_specs=[pl.BlockSpec(memory_space=pl.ANY)] * 7,
        out_specs=(vmem, vmem, vmem, vmem),
        scratch_shapes=scratch,
        compiler_params=pltpu.CompilerParams(
            collective_id=0, has_side_effects=True, vmem_limit_bytes=67043328
        ),
    )(*args)


def solution(mesh):
    both = P(("dp", "tp"), None)
    split = P("dp", "tp")
    return jax.shard_map(
        local_step,
        mesh=mesh,
        in_specs=(both, split, split, split, P(None, "tp"), P(None, "tp"), P(None, "tp")),
        out_specs=(both, split, split, split),
        check_vma=False,
    )
```

time: 390 us -> 108 us (0.28)
  waiting for transfers between devices: 332 us -> 0 us
  Pallas kernels: 0 us -> 99.8 us
  matrix products: 23.8 us -> 0 us
  between operations: 15.7 us -> 0.64 us
  local copies, waits for them, and re-layouts: 15.3 us -> 6.9 us
    all_gather x1 -> x0, waiting for transfers between devices: 159 us -> none  [local(): lax.all_gather(hidden, TP, axis=0, tiled=True)]
    unnamed x5 -> x0, waiting for transfers between devices: 136 us -> none
    pallas_call x0 -> x1, Pallas kernels: none -> 99.8 us  [local_step(): pl.pallas_call(kernel, out_shape=(jax.ShapeDtypeStruct((T, D), BF16), jax...]
    reduce_scatter x2 -> x0, waiting for transfers between devices: 37.9 us -> none  [scatter_axes(): nearer = lax.psum_scatter(array, axes[0], scatter_dimension=dim, tiled=True)]
    dot_general x2 -> x0, matrix products: 23.8 us -> none  [the longest x1 12.1 us: contract_rows(): lax.dot_general(left, right, (((0,), (0,)), ((), ())), preferred_element_...]
    unnamed x7 -> x4, local copies, waits for them, and re-layouts: 14.3 us -> 6.9 us
  transfers between devices with their start and end apart: 4 -> 0, of which waited for: 3 -> 0; matrix products, arithmetic and copies ran while one was open for 10% -> 0% of each run, Pallas kernels for 0% -> 0%
where the time goes in v1:
time: 108 us; the launch traced here: 107 us
  Pallas kernels  99.8 us (92%)
  local copies, waits for them, and re-layouts  6.9 us (6%)
    pallas_call x1, Pallas kernels, local_step(): pl.pallas_call(kernel, out_shape=(jax.ShapeDtypeStruct((T, D), BF16), jax...  99.8 us
    unnamed x4, local copies, waits for them, and re-layouts  6.9 us

profile of v1, /device:TPU:9, one launch (start us, length us, event | category | flops | bytes accessed | tf_op | source)
XLA Modules:
  0.0 107.4 jit_solution(431391787139355499)
XLA Ops:
  0.6 99.8 %shard_map.102 = (bf16[128,4096]{1,0:T(8,128)(2,1)}, f32[128,512]{1,0:T(8,128)}, f32[128,128]{1,0:T(8,128)}, f32[128,128]{1,0:T(8,128)}) custom-call(bf16[128,4096]{1,0:T(8,128)(2,1)} %hidden_ref.1, bf16[1024,512]{1,0:T(8,128)(2,1)} %q_ref.1, bf16[1024,128]{1,0:T(8,128)(2,1)} %k_ref.1, bf16[1024,128]{1,0:T(8,128)(2,1)} %v_ref.1, bf16[4096,512]{1,0:T(8,128)(2,1)} %wq_ref.1, ...), custom_call_target="tpu_custom_call" | custom-call | tf_op jit(solution)/shard_map/pallas_call | solution.py:445
  100.5 2.3 %copy.15 = bf16[128,4096]{1,0:T(8,128)(2,1)} copy(bf16[128,4096]{1,0:T(8,128)(2,1)} %get-tuple-element.8) | data formatting | bytes 2097152
  102.8 1.7 %copy.16 = f32[128,512]{1,0:T(8,128)} copy(f32[128,512]{1,0:T(8,128)} %get-tuple-element.9) | data formatting | bytes 524288
  104.4 1.5 %copy.17 = f32[128,128]{1,0:T(8,128)} copy(f32[128,128]{1,0:T(8,128)} %get-tuple-element.10) | data formatting | bytes 131072
  105.9 1.5 %copy.18 = f32[128,128]{1,0:T(8,128)} copy(f32[128,128]{1,0:T(8,128)} %get-tuple-element.11) | data formatting | bytes 131072

commit v2 on v1

--- a/solution.py
+++ b/solution.py
@@ -15,6 +15,7 @@
 CQ = 512
 CK = 128
 C = 768
+CW = 384
 
 
 def nt(left, right):
@@ -43,6 +44,7 @@
     goth,
     wmine,
     woth,
+    wt,
     wsend,
     hg,
     wg,
@@ -56,6 +58,8 @@
     yr,
     yos,
     yor,
+    os,
+    gs,
     lsem,
     ssem,
     rsem,
@@ -169,11 +173,11 @@
         for s in range(2)
     }
     o_y = remote(yos, yor, YI)
-    cc_copy = [remote(ccs.at[n], ccr.at[n], CC) for n in range(2)]
+    cc_copy = [remote(ccs.at[n], ccr.at[n], CC) for n in range(4)]
     steps = (pl.ds(0, 64), pl.ds(64, 128), pl.ds(192, 128), pl.ds(320, 128))
     zc = {
         (n, d, i): remote(zs.at[n, d, steps[i]], zr.at[n, d, steps[i]], ZP if d == 0 else ZM)
-        for n in range(2)
+        for n in range(4)
         for d in range(2)
         for i in range(4)
     }
@@ -204,18 +208,26 @@
 
         lax.fori_loop(0, 8, step, 0)
 
+    def turn(cc, ee, k):
+        piece = wpiece(cc, ee, k)
+        wt[:, piece] = woth[piece, :].T
+
     def hg_other(r):
         def step(n, carry):
-            cols = pl.ds(pl.multiple_of(n * 256, 256), 256)
-            hg[pl.ds(r * 256, 256), cols] += nt(goth[pl.ds(r * 256, 256), :], woth[cols, :])
+            cols = pl.ds(pl.multiple_of(n * 512, 512), 512)
+            block = pl.ds(r * 256, 256)
+            hg[block, cols] += jnp.dot(goth[block, :], wt[:, cols], preferred_element_type=F32)
             return carry
 
-        lax.fori_loop(0, 8, step, 0)
-
-    def wg_add(n, g, first, depth, fresh):
+        lax.fori_loop(0, 4, step, 0)
+
+    def wg_add(n, first, depth, fresh):
+        g = gown if n < 2 else goth
+        part_cols = pl.ds((n % 2) * CW, CW)
+
         def step(m, carry):
             cols = pl.ds(pl.multiple_of(m * 512, 512), 512)
-            part = tn(hid[pl.ds(first, depth), cols], g[pl.ds(first, depth), :])
+            part = tn(hid[pl.ds(first, depth), cols], g[pl.ds(first, depth), part_cols])
             if fresh:
                 wg[n, cols, :] = part
             else:
@@ -301,6 +313,26 @@
         hi = hg[block, right] + xr[0, 1, s].astype(F32) + xr[1, 2, s].astype(F32)
         return lo.astype(BF16), hi.astype(BF16)
 
+    def send_fin(n):
+        if n < 2:
+
+            @pl.when(yh != yl)
+            def _():
+                last[n].start()
+        else:
+            last[n].start()
+
+    last = [
+        remote(
+            fin.at[n],
+            yr.at[yh, n % 2],
+            dev(yhh=yl) if n < 2 else dev(yhh=yl, yll=1 - yl),
+            yssem.at[n],
+            yrsem.at[yh, n % 2],
+        )
+        for n in range(4)
+    ]
+
     hg_own()
     a_p[0].wait_recv()
     start(f_p[0])
@@ -314,108 +346,159 @@
     for i in range(2):
         start(b_p[i])
         start(b_m[1 - i])
+    turn(c, e, 0)
+    wg_add(0, 0, 256, True)
+    wg_add(1, 0, 256, True)
+    w_c[0].wait_recv()
+    turn(1 - c, e, 0)
     w_y[1].wait_recv()
     start(w_z[1])
     start(w_c[1])
     w_z[0].wait_recv()
     start(w_d[0])
+    turn(c, e, 1)
+    turn(c, 1 - e, 0)
     b_p[0].wait_recv()
     start(f_p[1])
     b_m[1].wait_recv()
     start(f_m[1])
+    w_c[1].wait_recv()
+    turn(1 - c, e, 1)
+    w_d[0].wait_recv()
+    turn(1 - c, 1 - e, 0)
     w_z[1].wait_recv()
     start(w_d[1])
+    turn(c, 1 - e, 1)
+    w_d[1].wait_recv()
+    turn(1 - c, 1 - e, 1)
+    g_y[3, 0].wait_recv()
+    g_y[3, 1].wait_recv()
+    hg_other(3)
+    x_far()
     a_p[1].wait_recv()
     a_m[0].wait_recv()
     b_p[1].wait_recv()
     b_m[0].wait_recv()
-    wg_add(0, gown, 0, 768, True)
-    for k in range(2):
-        w_c[k].wait_recv()
-        w_d[k].wait_recv()
-    g_y[3, 0].wait_recv()
-    g_y[3, 1].wait_recv()
-    hg_other(3)
-    x_far()
+    wg_add(0, 256, 512, False)
+    wg_add(1, 256, 512, False)
     for s in range(2):
         f_p[s].wait_recv()
         f_m[s].wait_recv()
-    wg_add(0, gown, 768, 256, False)
+    wg_add(0, 768, 256, False)
     cc_send(0)
-    for r in (1, 2):
-        g_y[r, 0].wait_recv()
-        g_y[r, 1].wait_recv()
-        hg_other(r)
-    x_direct(1)
+    wg_add(1, 768, 256, False)
+    cc_send(1)
+    g_y[1, 0].wait_recv()
+    g_y[1, 1].wait_recv()
+    hg_other(1)
     cc_copy[0].wait_recv()
     z_step(0, 0)
+    cc_copy[1].wait_recv()
+    z_step(1, 0)
+    g_y[2, 0].wait_recv()
+    g_y[2, 1].wait_recv()
+    hg_other(2)
+    x_direct(1)
     x_summed(1)
     x_direct(0)
     z_step(0, 1)
+    z_step(1, 1)
+    wg_add(2, 256, 768, True)
+    wg_add(3, 256, 768, True)
     g_y[0, 0].wait_recv()
     g_y[0, 1].wait_recv()
-    wg_add(1, goth, 0, 1024, True)
-    cc_send(1)
+    wg_add(2, 0, 256, False)
+    cc_send(2)
+    z_step(0, 2)
+    wg_add(3, 0, 256, False)
+    cc_send(3)
+    z_step(1, 2)
     x_summed(0)
+    cc_copy[2].wait_recv()
+    z_step(2, 0)
+    cc_copy[3].wait_recv()
+    z_step(3, 0)
     hg_other(0)
-    cc_copy[1].wait_recv()
-    z_step(1, 0)
-    z_step(0, 2)
-    z_step(1, 1)
+    z_step(0, 3)
+    z_step(1, 3)
+    z_step(2, 1)
+    z_step(3, 1)
     lo, hi = x_total(1)
     yos[:, left] = lo
     yos[:, right] = hi
     start(o_y)
-    z_step(0, 3)
-    z_step(1, 2)
     z_last(0)
-
-    own_copy = remote(fin.at[0], yr.at[yh], dev(yhh=yl), yssem.at[0], yrsem.at[yh])
-    other_copy = remote(fin.at[1], yr.at[yh], dev(yhh=yl, yll=1 - yl), yssem.at[1], yrsem.at[yh])
+    send_fin(0)
+    z_last(1)
+    send_fin(1)
+    z_step(2, 2)
+    z_step(3, 2)
+    z_step(2, 3)
+    z_step(3, 3)
+    lo, hi = x_total(0)
+    os[:, left] = lo
+    os[:, right] = hi
+    put_mine = local(os, out_ref.at[:, mine], 5)
+    o_y.wait_recv()
+    put_other = local(yor, out_ref.at[:, other], 6)
+    z_last(2)
+    send_fin(2)
+    z_last(3)
+    send_fin(3)
+
+    def arrived(slot, n):
+        pltpu.make_async_copy(yr.at[slot, n], yr.at[slot, n], yrsem.at[slot, n]).wait()
+
+    for n in range(2):
+        chunk = pl.ds(n * CW, CW)
+
+        @pl.when(yh == yl)
+        def _():
+            arrived(1 - yh, n)
+            gs[:, chunk] = fin[n].astype(F32) + yr[1 - yh, n].astype(F32)
+
+        @pl.when(yh != yl)
+        def _():
+            arrived(0, n)
+            arrived(1, n)
+            gs[:, chunk] = yr[0, n].astype(F32) + yr[1, n].astype(F32)
+
+    puts = [
+        local(gs.at[:, pl.ds(0, CQ)], gq_ref, 7),
+        local(gs.at[:, pl.ds(CQ, CK)], gk_ref, 8),
+        local(gs.at[:, pl.ds(CQ + CK, CK)], gv_ref, 9),
+    ]
 
     @pl.when(yh != yl)
     def _():
-        own_copy.start()
-
-    z_step(1, 3)
-    lo, hi = x_total(0)
-    out_ref[:, pl.ds(pl.multiple_of(yl * H, H), HH)] = lo
-    out_ref[:, pl.ds(pl.multiple_of(yl * H + HH, HH), HH)] = hi
-    o_y.wait_recv()
-    out_ref[:, pl.ds(pl.multiple_of((1 - yl) * H, H), H)] = yor[...]
-    z_last(1)
-    other_copy.start()
-
-    def finish(total):
-        gq_ref[...] = total[:, :CQ]
-        gk_ref[...] = total[:, CQ : CQ + CK]
-        gv_ref[...] = total[:, CQ + CK :]
-
-    def arrived(slot):
-        pltpu.make_async_copy(yr.at[slot], yr.at[slot], yrsem.at[slot]).wait()
-
-    @pl.when(yh == yl)
-    def _():
-        arrived(1 - yh)
-        finish(fin[0].astype(F32) + yr[1 - yh].astype(F32))
-
-    @pl.when(yh != yl)
-    def _():
-        arrived(0)
-        arrived(1)
-        finish(yr[0].astype(F32) + yr[1].astype(F32))
-        own_copy.wait_send()
-
-    other_copy.wait_send()
+        last[0].wait_send()
+        last[1].wait_send()
+
+    last[2].wait_send()
+    last[3].wait_send()
     for copy in sent:
         copy.wait_send()
-
-
-N_SEM = 80
+    for put in [put_mine, put_other] + puts:
+        put.wait()
+
+
+def hand_over(*refs):
+    sources, targets, through, (into, out) = refs[:4], refs[4:8], refs[8:12], refs[12:]
+    loads = [pltpu.make_async_copy(sources[i], through[i], into.at[i]) for i in range(4)]
+    stores = [pltpu.make_async_copy(through[i], targets[i], out.at[i]) for i in range(4)]
+    for load in loads:
+        load.start()
+    for load, store in zip(loads, stores):
+        load.wait()
+        store.start()
+    for store in stores:
+        store.wait()
+
+
+N_SEM = 96
 
 
 def local_step(*args):
-    vmem = pl.BlockSpec(memory_space=pltpu.VMEM)
     scratch = [
         pltpu.VMEM((1024, H), BF16),
         pltpu.VMEM((T, H), BF16),
@@ -423,40 +506,50 @@
         pltpu.VMEM((1024, C), BF16),
         pltpu.VMEM((H, C), BF16),
         pltpu.VMEM((H, C), BF16),
+        pltpu.VMEM((C, H), BF16),
         pltpu.VMEM((512, C), BF16),
         pltpu.VMEM((1024, H), F32),
-        pltpu.VMEM((2, H, C), F32),
-        pltpu.VMEM((2, 1024, C), BF16),
-        pltpu.VMEM((2, 1024, C), BF16),
+        pltpu.VMEM((4, H, CW), F32),
+        pltpu.VMEM((4, 1024, CW), BF16),
+        pltpu.VMEM((4, 1024, CW), BF16),
         pltpu.VMEM((2, 3, 2, T, HH), BF16),
         pltpu.VMEM((2, 3, 2, T, HH), BF16),
-        pltpu.VMEM((2, 2, 448, C), BF16),
-        pltpu.VMEM((2, 2, 448, C), BF16),
-        pltpu.VMEM((2, T, C), BF16),
-        pltpu.VMEM((2, T, C), BF16),
+        pltpu.VMEM((4, 2, 448, CW), BF16),
+        pltpu.VMEM((4, 2, 448, CW), BF16),
+        pltpu.VMEM((4, T, CW), BF16),
+        pltpu.VMEM((2, 2, T, CW), BF16),
         pltpu.VMEM((T, H), BF16),
         pltpu.VMEM((T, H), BF16),
-        pltpu.SemaphoreType.DMA((5,)),
+        pltpu.VMEM((T, H), BF16),
+        pltpu.VMEM((T, C), F32),
+        pltpu.SemaphoreType.DMA((10,)),
         pltpu.SemaphoreType.DMA((N_SEM,)),
         pltpu.SemaphoreType.DMA((N_SEM,)),
-        pltpu.SemaphoreType.DMA((2,)),
-        pltpu.SemaphoreType.DMA((2,)),
+        pltpu.SemaphoreType.DMA((4,)),
+        pltpu.SemaphoreType.DMA((2, 2)),
     ]
-    return pl.pallas_call(
+    anywhere = pl.BlockSpec(memory_space=pl.ANY)
+    shapes = [((T, D), BF16), ((T, CQ), F32), ((T, CK), F32), ((T, CK), F32)]
+    out_shape = tuple(jax.ShapeDtypeStruct(*shape) for shape in shapes)
+    results = pl.pallas_call(
         kernel,
-        out_shape=(
-            jax.ShapeDtypeStruct((T, D), BF16),
-            jax.ShapeDtypeStruct((T, CQ), F32),
-            jax.ShapeDtypeStruct((T, CK), F32),
-            jax.ShapeDtypeStruct((T, CK), F32),
-        ),
-        in_specs=[pl.BlockSpec(memory_space=pl.ANY)] * 7,
-        out_specs=(vmem, vmem, vmem, vmem),
+        out_shape=out_shape,
+        in_specs=[anywhere] * 7,
+        out_specs=(anywhere,) * 4,
         scratch_shapes=scratch,
         compiler_params=pltpu.CompilerParams(
             collective_id=0, has_side_effects=True, vmem_limit_bytes=67043328
         ),
     )(*args)
+    return pl.pallas_call(
+        hand_over,
+        out_shape=out_shape,
+        in_specs=[anywhere] * 4,
+        out_specs=(anywhere,) * 4,
+        scratch_shapes=[pltpu.VMEM(*shape) for shape in shapes]
+        + [pltpu.SemaphoreType.DMA((4,)), pltpu.SemaphoreType.DMA((4,))],
+        cost_estimate=pl.CostEstimate(flops=0, bytes_accessed=3 << 20, transcendentals=0),
+    )(*results)
 
 
 def solution(mesh):

time: 108 us -> 96.1 us (0.89)
  local copies, waits for them, and re-layouts: 6.9 us -> 0 us
  Pallas kernels: 99.8 us -> 94.7 us
    unnamed x4 -> x0, local copies, waits for them, and re-layouts: 6.9 us -> none
    pallas_call x1 -> x2, Pallas kernels: 99.8 us -> 94.7 us  [the longest x1 92.3 us: local_step(): pl.pallas_call(kernel, out_shape=out_shape, in_specs=[anywhere] * 7, out_...]
where the time goes in v2:
time: 96.1 us; the launch traced here: 95.3 us
  Pallas kernels  94.7 us (99%)
    pallas_call x1, Pallas kernels, local_step(): pl.pallas_call(kernel, out_shape=out_shape, in_specs=[anywhere] * 7, out_...  92.3 us
    pallas_call x1, Pallas kernels, local_step(): pl.pallas_call(hand_over, out_shape=out_shape, in_specs=[anywhere] * 4, o...  2.38 us

profile of v2, /device:TPU:9, one launch (start us, length us, event | category | flops | bytes accessed | tf_op | source)
XLA Modules:
  0.0 95.3 jit_solution(15969967638830758561)
XLA Ops:
  0.6 92.3 %shard_map.102 = (bf16[128,4096]{1,0:T(8,128)(2,1)}, f32[128,512]{1,0:T(8,128)}, f32[128,128]{1,0:T(8,128)}, f32[128,128]{1,0:T(8,128)}) custom-call(bf16[128,4096]{1,0:T(8,128)(2,1)} %hidden_ref.1, bf16[1024,512]{1,0:T(8,128)(2,1)} %q_ref.1, bf16[1024,128]{1,0:T(8,128)(2,1)} %k_ref.1, bf16[1024,128]{1,0:T(8,128)(2,1)} %v_ref.1, bf16[4096,512]{1,0:T(8,128)(2,1)} %wq_ref.1, ...), custom_call_target="tpu_custom_call" | custom-call | tf_op jit(solution)/shard_map/pallas_call | solution.py:534
  92.9 2.4 %shard_map.103 = (bf16[128,4096]{1,0:T(8,128)(2,1)}, f32[128,512]{1,0:T(8,128)}, f32[128,128]{1,0:T(8,128)}, f32[128,128]{1,0:T(8,128)}) custom-call(bf16[128,4096]{1,0:T(8,128)(2,1)} %get-tuple-element.8.refs_0_, f32[128,512]{1,0:T(8,128)} %get-tuple-element.9.refs_1_, f32[128,128]{1,0:T(8,128)} %get-tuple-element.10.refs_2_, ...), custom_call_target="tpu_custom_call" | custom-call | bytes 3145728 | tf_op jit(solution)/shard_map/pallas_call | solution.py:544

commit v3 on v2

--- a/solution.py
+++ b/solution.py
@@ -42,7 +42,7 @@
     hsend,
     gown,
     goth,
-    wmine,
+    wh,
     woth,
     wt,
     wsend,
@@ -108,7 +108,8 @@
 
     def start(copy):
         copy.start()
-        sent.append(copy)
+        if not any(copy is one for one in sent):
+            sent.append(copy)
 
     def local(src, dst, i):
         copy = pltpu.make_async_copy(src, dst, lsem.at[i])
@@ -117,8 +118,14 @@
 
     mine = pl.ds(pl.multiple_of(yl * H, H), H)
     other = pl.ds(pl.multiple_of((1 - yl) * H, H), H)
-    load_a = local(hidden_ref.at[:, mine], hid.at[pl.ds(0, T)], 0)
-    load_b = local(hidden_ref.at[:, other], hsend, 1)
+    for h in range(2):
+        for zz in range(8):
+            first = pl.multiple_of(yl * H + (2 * zz + h) * T, T)
+            local(hidden_ref.at[:, pl.ds(first, T)], hid.at[h, zz, pl.ds(0, T)], 0 if h == 0 else 10)
+    for h in range(2):
+        for zz in range(8):
+            first = pl.multiple_of((1 - yl) * H + (2 * zz + h) * T, T)
+            local(hidden_ref.at[:, pl.ds(first, T)], hsend.at[h, zz], 1)
     wrow = c * 1024 + e * 512
     wrows = pl.ds(pl.multiple_of((1 - yl) * H + wrow, 512), 512)
     local(wq_ref.at[wrows], wsend.at[:, pl.ds(0, CQ)], 2)
@@ -132,9 +139,9 @@
             local(q_ref.at[src], gown.at[dst, pl.ds(0, CQ)], 3)
             local(k_ref.at[src], gown.at[dst, pl.ds(CQ, CK)], 3)
             local(v_ref.at[src], gown.at[dst, pl.ds(CQ + CK, CK)], 3)
-    local(wq_ref.at[mine], wmine.at[:, pl.ds(0, CQ)], 4)
-    local(wk_ref.at[mine], wmine.at[:, pl.ds(CQ, CK)], 4)
-    local(wv_ref.at[mine], wmine.at[:, pl.ds(CQ + CK, CK)], 4)
+    local(wq_ref.at[mine], wh.at[:, pl.ds(0, CQ)], 4)
+    local(wk_ref.at[mine], wh.at[:, pl.ds(CQ, CK)], 4)
+    local(wv_ref.at[mine], wh.at[:, pl.ds(CQ + CK, CK)], 4)
 
     def wait_local(buffer, i):
         pltpu.make_async_copy(buffer, buffer, lsem.at[i]).wait()
@@ -148,13 +155,17 @@
         first = r * 256 + s * T
         return pl.ds(first, T) if half is None else pl.ds(first + half * 64, 64)
 
-    a_p = [remote(hid.at[rows(0, 0, i)], hid.at[rows(2, 0, i)], XP) for i in range(2)]
-    a_m = [remote(hid.at[rows(0, 0, i)], hid.at[rows(1, 0, i)], XM) for i in range(2)]
-    b_y = [remote(hsend.at[pl.ds(64 * i, 64)], hid.at[rows(0, 1, i)], YI) for i in range(2)]
-    b_p = [remote(hid.at[rows(0, 1, i)], hid.at[rows(2, 1, i)], XP) for i in range(2)]
-    b_m = [remote(hid.at[rows(0, 1, i)], hid.at[rows(1, 1, i)], XM) for i in range(2)]
-    f_p = [remote(hid.at[rows(2, s, 0)], hid.at[rows(3, s, 0)], XP) for s in range(2)]
-    f_m = [remote(hid.at[rows(1, s, 1)], hid.at[rows(3, s, 1)], XM) for s in range(2)]
+    def piece(h, r, s, i):
+        return hid.at[h, :, rows(r, s, i)]
+
+    both = range(2)
+    a_p = [[remote(piece(h, 0, 0, i), piece(h, 2, 0, i), XP) for i in both] for h in both]
+    a_m = [[remote(piece(h, 0, 0, i), piece(h, 1, 0, i), XM) for i in both] for h in both]
+    b_y = [remote(hsend.at[h], hid.at[h, :, rows(0, 1)], YI) for h in both]
+    b_p = [[remote(piece(h, 0, 1, i), piece(h, 2, 1, i), XP) for i in both] for h in both]
+    b_m = [[remote(piece(h, 0, 1, i), piece(h, 1, 1, i), XM) for i in both] for h in both]
+    f_p = [[remote(piece(h, 2, s, 0), piece(h, 3, s, 0), XP) for s in both] for h in both]
+    f_m = [[remote(piece(h, 1, s, 1), piece(h, 3, s, 1), XM) for s in both] for h in both]
     g_y = {
         (r, s): remote(gown.at[rows(r, s)], goth.at[rows(r, 1 - s)], YI) for r in (3, 1, 2, 0) for s in range(2)
     }
@@ -182,13 +193,12 @@
         for i in range(4)
     }
 
-    load_a.wait()
+    wait_local(hid.at[0, :, pl.ds(0, T)], 0)
     for i in range(2):
-        start(a_p[i])
-        start(a_m[1 - i])
-    load_b.wait()
-    for i in range(2):
-        start(b_y[i])
+        start(a_p[0][i])
+        start(a_m[0][1 - i])
+    wait_local(hsend, 1)
+    start(b_y[0])
     wait_local(wsend, 2)
     for k in range(2):
         start(w_y[k])
@@ -196,12 +206,15 @@
     for r in (3, 1, 2, 0):
         for s in (0, 1):
             start(g_y[r, s])
-    wait_local(wmine, 4)
+        if r == 3:
+            start(b_y[1])
+    wait_local(hid.at[1, :, pl.ds(0, T)], 10)
+    wait_local(wh.at[:, pl.ds(0, C)], 4)
 
     def hg_own():
         def step(n, carry):
             cols = pl.ds(pl.multiple_of(n * 256, 256), 256)
-            w = wmine[cols, :]
+            w = wh[cols, :C]
             for m in range(2):
                 hg[pl.ds(m * 512, 512), cols] = nt(gown[pl.ds(m * 512, 512), :], w)
             return carry
@@ -221,35 +234,62 @@
 
         lax.fori_loop(0, 4, step, 0)
 
-    def wg_add(n, first, depth, fresh):
-        g = gown if n < 2 else goth
-        part_cols = pl.ds((n % 2) * CW, CW)
+    def flip(h, r):
+        def step(zz, carry):
+            dst = pl.ds(pl.multiple_of(h * 1024 + zz * T, T), T)
+            block = pl.ds(r * 256, 256)
+            wh[dst, block] = hid[h, zz, block, :].T
+            return carry
+
+        lax.fori_loop(0, 8, step, 0)
+
+    def wg_add(pair, h, first, depth, fresh):
+        g = goth if pair else gown
+        toks = pl.ds(first, depth)
 
         def step(m, carry):
-            cols = pl.ds(pl.multiple_of(m * 512, 512), 512)
-            part = tn(hid[pl.ds(first, depth), cols], g[pl.ds(first, depth), part_cols])
-            if fresh:
-                wg[n, cols, :] = part
-            else:
-                wg[n, cols, :] += part
+            block = pl.ds(pl.multiple_of(h * 1024 + m * 512, 512), 512)
+            part = jnp.dot(wh[block, toks], g[toks, :], preferred_element_type=F32)
+            for i in range(2):
+                cut = part[:, i * CW : (i + 1) * CW]
+                wg[2 * pair + i, block, :] = cut if fresh else wg[2 * pair + i, block, :] + cut
             return carry
 
-        lax.fori_loop(0, 4, step, 0)
-
-    def cc_send(n):
-        def step(zz, carry):
-            src = pl.ds(pl.multiple_of((2 * zz + 1 - c) * T, T), T)
-            dst = pl.ds(pl.multiple_of(zz * T, T), T)
-            ccs[n, dst, :] = wg[n, src, :].astype(BF16)
-            return carry
-
-        lax.fori_loop(0, 8, step, 0)
-        start(cc_copy[n])
+        lax.fori_loop(0, 2, step, 0)
+
+    def cc_send(n, h):
+        @pl.when(c != h)
+        def _():
+            for m in range(4):
+                ccs[n, pl.ds(m * 256, 256), :] = wg[n, pl.ds(h * 1024 + m * 256, 256), :].astype(BF16)
+            start(cc_copy[n])
 
     def pair_sum(n, zz, first=0, size=T):
-        src = pl.ds(pl.multiple_of((2 * zz + c) * T + first, size), size)
+        src = pl.ds(pl.multiple_of(c * 1024 + zz * T + first, size), size)
         dst = pl.ds(pl.multiple_of(zz * T + first, size), size)
         return wg[n, src, :] + ccr[n, dst, :].astype(F32)
+
+    def z_own(i):
+        for n in range(2):
+            z_any(n, i)
+
+    def z_other(i):
+        for n in range(2, 4):
+            z_any(n, i)
+
+    def z_any(n, i):
+        if i == 0:
+            cc_copy[n].wait_recv()
+        if i < 4:
+            z_step(n, i)
+        else:
+            z_last(n)
+            send_fin(n)
+
+    def on_core(h, work, *args):
+        @pl.when(c == h)
+        def _():
+            work(*args)
 
     def z_step(n, i):
         if i == 0:
@@ -333,35 +373,71 @@
         for n in range(4)
     ]
 
+    def hid_in(h, r):
+        if r == 3:
+            for s in range(2):
+                f_p[h][s].wait_recv()
+                f_m[h][s].wait_recv()
+        else:
+            copies = (a_p[h], b_p[h]) if r == 2 else (a_m[h], b_m[h])
+            i = 1 if r == 2 else 0
+            for copy in copies:
+                copy[i].wait_recv()
+
+    def forward(h, s):
+        src_p, src_m = (b_p, b_m) if s else (a_p, a_m)
+        src_p[h][0].wait_recv()
+        start(f_p[h][s])
+        src_m[h][1].wait_recv()
+        start(f_m[h][s])
+
+    def send_b(h):
+        b_y[h].wait_recv()
+        for i in range(2):
+            start(b_p[h][i])
+            start(b_m[h][1 - i])
+
+    def g_in(r):
+        g_y[r, 0].wait_recv()
+        g_y[r, 1].wait_recv()
+
     hg_own()
-    a_p[0].wait_recv()
-    start(f_p[0])
-    a_m[1].wait_recv()
-    start(f_m[0])
+    forward(0, 0)
+    send_b(0)
+    flip(0, 0)
+    wg_add(0, 0, 0, 256, True)
     w_y[0].wait_recv()
     start(w_z[0])
     start(w_c[0])
+    forward(0, 1)
     for i in range(2):
-        b_y[i].wait_recv()
-    for i in range(2):
-        start(b_p[i])
-        start(b_m[1 - i])
+        start(a_p[1][i])
+        start(a_m[1][1 - i])
     turn(c, e, 0)
-    wg_add(0, 0, 256, True)
-    wg_add(1, 0, 256, True)
-    w_c[0].wait_recv()
-    turn(1 - c, e, 0)
+    hid_in(0, 1)
+    hid_in(0, 2)
+    flip(0, 1)
+    flip(0, 2)
+    wg_add(0, 0, 256, 512, False)
     w_y[1].wait_recv()
     start(w_z[1])
     start(w_c[1])
+    w_c[0].wait_recv()
+    turn(1 - c, e, 0)
+    hid_in(0, 3)
+    flip(0, 3)
+    wg_add(0, 0, 768, 256, False)
+    cc_send(0, 0)
+    cc_send(1, 0)
     w_z[0].wait_recv()
     start(w_d[0])
+    forward(1, 0)
+    send_b(1)
+    on_core(0, z_own, 0)
     turn(c, e, 1)
     turn(c, 1 - e, 0)
-    b_p[0].wait_recv()
-    start(f_p[1])
-    b_m[1].wait_recv()
-    start(f_m[1])
+    flip(1, 0)
+    wg_add(0, 1, 0, 256, True)
     w_c[1].wait_recv()
     turn(1 - c, e, 1)
     w_d[0].wait_recv()
@@ -369,82 +445,63 @@
     w_z[1].wait_recv()
     start(w_d[1])
     turn(c, 1 - e, 1)
+    g_in(3)
     w_d[1].wait_recv()
     turn(1 - c, 1 - e, 1)
-    g_y[3, 0].wait_recv()
-    g_y[3, 1].wait_recv()
+    on_core(0, z_own, 1)
     hg_other(3)
+    forward(1, 1)
     x_far()
-    a_p[1].wait_recv()
-    a_m[0].wait_recv()
-    b_p[1].wait_recv()
-    b_m[0].wait_recv()
-    wg_add(0, 256, 512, False)
-    wg_add(1, 256, 512, False)
-    for s in range(2):
-        f_p[s].wait_recv()
-        f_m[s].wait_recv()
-    wg_add(0, 768, 256, False)
-    cc_send(0)
-    wg_add(1, 768, 256, False)
-    cc_send(1)
-    g_y[1, 0].wait_recv()
-    g_y[1, 1].wait_recv()
+    hid_in(1, 1)
+    hid_in(1, 2)
+    on_core(0, z_own, 2)
+    flip(1, 1)
+    flip(1, 2)
+    wg_add(0, 1, 256, 512, False)
+    hid_in(1, 3)
+    flip(1, 3)
+    wg_add(0, 1, 768, 256, False)
+    cc_send(0, 1)
+    cc_send(1, 1)
+    g_in(1)
     hg_other(1)
-    cc_copy[0].wait_recv()
-    z_step(0, 0)
-    cc_copy[1].wait_recv()
-    z_step(1, 0)
-    g_y[2, 0].wait_recv()
-    g_y[2, 1].wait_recv()
+    g_in(2)
     hg_other(2)
     x_direct(1)
+    on_core(1, z_own, 0)
+    wg_add(1, 0, 256, 768, True)
+    on_core(0, z_own, 3)
     x_summed(1)
     x_direct(0)
-    z_step(0, 1)
-    z_step(1, 1)
-    wg_add(2, 256, 768, True)
-    wg_add(3, 256, 768, True)
-    g_y[0, 0].wait_recv()
-    g_y[0, 1].wait_recv()
-    wg_add(2, 0, 256, False)
-    cc_send(2)
-    z_step(0, 2)
-    wg_add(3, 0, 256, False)
-    cc_send(3)
-    z_step(1, 2)
+    on_core(1, z_own, 1)
+    wg_add(1, 1, 256, 768, True)
+    g_in(0)
+    for h in range(2):
+        wg_add(1, h, 0, 256, False)
+        cc_send(2, h)
+        cc_send(3, h)
+    on_core(0, z_own, 4)
+    on_core(1, z_own, 2)
     x_summed(0)
-    cc_copy[2].wait_recv()
-    z_step(2, 0)
-    cc_copy[3].wait_recv()
-    z_step(3, 0)
+    z_other(0)
     hg_other(0)
-    z_step(0, 3)
-    z_step(1, 3)
-    z_step(2, 1)
-    z_step(3, 1)
+    on_core(1, z_own, 3)
+    z_other(1)
+    on_core(1, z_own, 4)
     lo, hi = x_total(1)
     yos[:, left] = lo
     yos[:, right] = hi
     start(o_y)
-    z_last(0)
-    send_fin(0)
-    z_last(1)
-    send_fin(1)
-    z_step(2, 2)
-    z_step(3, 2)
-    z_step(2, 3)
-    z_step(3, 3)
+    z_other(2)
+    z_other(3)
+    z_any(2, 4)
     lo, hi = x_total(0)
     os[:, left] = lo
     os[:, right] = hi
     put_mine = local(os, out_ref.at[:, mine], 5)
+    z_any(3, 4)
     o_y.wait_recv()
     put_other = local(yor, out_ref.at[:, other], 6)
-    z_last(2)
-    send_fin(2)
-    z_last(3)
-    send_fin(3)
 
     def arrived(slot, n):
         pltpu.make_async_copy(yr.at[slot, n], yr.at[slot, n], yrsem.at[slot, n]).wait()
@@ -500,11 +557,11 @@
 
 def local_step(*args):
     scratch = [
-        pltpu.VMEM((1024, H), BF16),
-        pltpu.VMEM((T, H), BF16),
+        pltpu.VMEM((2, 8, 1024, T), BF16),
+        pltpu.VMEM((2, 8, T, T), BF16),
         pltpu.VMEM((1024, C), BF16),
         pltpu.VMEM((1024, C), BF16),
-        pltpu.VMEM((H, C), BF16),
+        pltpu.VMEM((H, 1024), BF16),
         pltpu.VMEM((H, C), BF16),
         pltpu.VMEM((C, H), BF16),
         pltpu.VMEM((512, C), BF16),
@@ -522,7 +579,7 @@
         pltpu.VMEM((T, H), BF16),
         pltpu.VMEM((T, H), BF16),
         pltpu.VMEM((T, C), F32),
-        pltpu.SemaphoreType.DMA((10,)),
+        pltpu.SemaphoreType.DMA((11,)),
         pltpu.SemaphoreType.DMA((N_SEM,)),
         pltpu.SemaphoreType.DMA((N_SEM,)),
         pltpu.SemaphoreType.DMA((4,)),

time: 96.1 us -> 90 us (0.937)
  Pallas kernels: 94.7 us -> 88.4 us
    pallas_call x1, Pallas kernels: 92.3 us -> 86.1 us  [local_step(): pl.pallas_call(kernel, out_shape=out_shape, in_specs=[anywhere] * 7, out_...]
where the time goes in v3:
time: 90 us; the launch traced here: 89.1 us
  Pallas kernels  88.4 us (98%)
    pallas_call x1, Pallas kernels, local_step(): pl.pallas_call(kernel, out_shape=out_shape, in_specs=[anywhere] * 7, out_...  86.1 us
    pallas_call x1, Pallas kernels, local_step(): pl.pallas_call(hand_over, out_shape=out_shape, in_specs=[anywhere] * 4, o...  2.38 us

profile of v3, /device:TPU:9, one launch (start us, length us, event | category | flops | bytes accessed | tf_op | source)
XLA Modules:
  0.0 89.1 jit_solution(3476142368020095597)
XLA Ops:
  0.6 86.1 %shard_map.102 = (bf16[128,4096]{1,0:T(8,128)(2,1)}, f32[128,512]{1,0:T(8,128)}, f32[128,128]{1,0:T(8,128)}, f32[128,128]{1,0:T(8,128)}) custom-call(bf16[128,4096]{1,0:T(8,128)(2,1)} %hidden_ref.1, bf16[1024,512]{1,0:T(8,128)(2,1)} %q_ref.1, bf16[1024,128]{1,0:T(8,128)(2,1)} %k_ref.1, bf16[1024,128]{1,0:T(8,128)(2,1)} %v_ref.1, bf16[4096,512]{1,0:T(8,128)(2,1)} %wq_ref.1, ...), custom_call_target="tpu_custom_call" | custom-call | tf_op jit(solution)/shard_map/pallas_call | solution.py:591
  86.7 2.4 %shard_map.103 = (bf16[128,4096]{1,0:T(8,128)(2,1)}, f32[128,512]{1,0:T(8,128)}, f32[128,128]{1,0:T(8,128)}, f32[128,128]{1,0:T(8,128)}) custom-call(bf16[128,4096]{1,0:T(8,128)(2,1)} %get-tuple-element.8.refs_0_, f32[128,512]{1,0:T(8,128)} %get-tuple-element.9.refs_1_, f32[128,128]{1,0:T(8,128)} %get-tuple-element.10.refs_2_, ...), custom_call_target="tpu_custom_call" | custom-call | bytes 3145728 | tf_op jit(solution)/shard_map/pallas_call | solution.py:601

commit v4 on v3

--- a/solution.py
+++ b/solution.py
@@ -15,7 +15,9 @@
 CQ = 512
 CK = 128
 C = 768
-CW = 384
+CHUNKS = ((0, 0, 384), (0, 384, 384), (1, 0, 256), (1, 256, 256), (1, 512, 256))
+OWN = (0, 1)
+PAIR = (2, 3, 4)
 
 
 def nt(left, right):
@@ -35,9 +37,7 @@
     wk_ref,
     wv_ref,
     out_ref,
-    gq_ref,
-    gk_ref,
-    gv_ref,
+    yr,
     hid,
     hsend,
     gown,
@@ -55,11 +55,8 @@
     zs,
     zr,
     fin,
-    yr,
     yos,
-    yor,
     os,
-    gs,
     lsem,
     ssem,
     rsem,
@@ -171,27 +168,31 @@
     }
 
     def wpiece(cc, ee, k):
-        return pl.ds(pl.multiple_of(cc * 1024 + ee * 512 + k * 256, 256), 256)
-
-    w_y = [remote(wsend.at[pl.ds(256 * k, 256)], woth.at[wpiece(c, e, k)], YO) for k in range(2)]
-    w_z = [remote(woth.at[wpiece(c, e, k)], woth.at[wpiece(c, e, k)], ZX) for k in range(2)]
-    w_c = [remote(woth.at[wpiece(c, e, k)], woth.at[wpiece(c, e, k)], CC) for k in range(2)]
-    w_d = [remote(woth.at[wpiece(c, 1 - e, k)], woth.at[wpiece(c, 1 - e, k)], CC) for k in range(2)]
+        return pl.ds(pl.multiple_of(cc * 1024 + ee * 512 + k * 128, 128), 128)
+
+    w_y = [remote(wsend.at[pl.ds(128 * k, 128)], woth.at[wpiece(c, e, k)], YO) for k in range(4)]
+    w_z = [remote(woth.at[wpiece(c, e, k)], woth.at[wpiece(c, e, k)], ZX) for k in range(4)]
+    w_c = [remote(woth.at[wpiece(c, e, k)], woth.at[wpiece(c, e, k)], CC) for k in range(4)]
+    w_d = [remote(woth.at[wpiece(c, 1 - e, k)], woth.at[wpiece(c, 1 - e, k)], CC) for k in range(4)]
     xc = {
         (d, b, s): remote(xs.at[d, b, s], xr.at[d, b, s], XP if d == 0 else XM)
         for d in range(2)
         for b in range(3)
         for s in range(2)
     }
-    o_y = remote(yos, yor, YI)
-    cc_copy = [remote(ccs.at[n], ccr.at[n], CC) for n in range(4)]
+    o_y = remote(yos, out_ref.at[:, mine], YI)
+    cc_copy = []
+    for n, (p, first, width) in enumerate(CHUNKS):
+        cols = pl.ds(first, width)
+        cc_copy.append(remote(ccs.at[p, :, cols], ccr.at[p, :, cols], CC))
     steps = (pl.ds(0, 64), pl.ds(64, 128), pl.ds(192, 128), pl.ds(320, 128))
-    zc = {
-        (n, d, i): remote(zs.at[n, d, steps[i]], zr.at[n, d, steps[i]], ZP if d == 0 else ZM)
-        for n in range(4)
-        for d in range(2)
-        for i in range(4)
-    }
+    zc = {}
+    for n, (p, first, width) in enumerate(CHUNKS):
+        cols = pl.ds(first, width)
+        for d in range(2):
+            for i in range(4):
+                part = (p, d, steps[i], cols)
+                zc[n, d, i] = remote(zs.at[part], zr.at[part], ZP if d == 0 else ZM)
 
     wait_local(hid.at[0, :, pl.ds(0, T)], 0)
     for i in range(2):
@@ -200,7 +201,7 @@
     wait_local(hsend, 1)
     start(b_y[0])
     wait_local(wsend, 2)
-    for k in range(2):
+    for k in range(4):
         start(w_y[k])
     wait_local(gown, 3)
     for r in (3, 1, 2, 0):
@@ -225,10 +226,11 @@
         piece = wpiece(cc, ee, k)
         wt[:, piece] = woth[piece, :].T
 
-    def hg_other(r):
+    def hg_other(r, s=None):
+        block = pl.ds(r * 256, 256) if s is None else pl.ds(r * 256 + s * T, T)
+
         def step(n, carry):
             cols = pl.ds(pl.multiple_of(n * 512, 512), 512)
-            block = pl.ds(r * 256, 256)
             hg[block, cols] += jnp.dot(goth[block, :], wt[:, cols], preferred_element_type=F32)
             return carry
 
@@ -250,31 +252,35 @@
         def step(m, carry):
             block = pl.ds(pl.multiple_of(h * 1024 + m * 512, 512), 512)
             part = jnp.dot(wh[block, toks], g[toks, :], preferred_element_type=F32)
-            for i in range(2):
-                cut = part[:, i * CW : (i + 1) * CW]
-                wg[2 * pair + i, block, :] = cut if fresh else wg[2 * pair + i, block, :] + cut
+            wg[pair, block, :] = part if fresh else wg[pair, block, :] + part
             return carry
 
         lax.fori_loop(0, 2, step, 0)
 
-    def cc_send(n, h):
+    def cc_send(chunks, h):
         @pl.when(c != h)
         def _():
-            for m in range(4):
-                ccs[n, pl.ds(m * 256, 256), :] = wg[n, pl.ds(h * 1024 + m * 256, 256), :].astype(BF16)
-            start(cc_copy[n])
-
-    def pair_sum(n, zz, first=0, size=T):
-        src = pl.ds(pl.multiple_of(c * 1024 + zz * T + first, size), size)
-        dst = pl.ds(pl.multiple_of(zz * T + first, size), size)
-        return wg[n, src, :] + ccr[n, dst, :].astype(F32)
+            for n in chunks:
+                p, first, width = CHUNKS[n]
+                cols = pl.ds(first, width)
+                for m in range(4):
+                    src = pl.ds(h * 1024 + m * 256, 256)
+                    ccs[p, pl.ds(m * 256, 256), cols] = wg[p, src, cols].astype(BF16)
+                start(cc_copy[n])
+
+    def pair_sum(n, zz, start_row=0, size=T):
+        p, first, width = CHUNKS[n]
+        cols = pl.ds(first, width)
+        src = pl.ds(pl.multiple_of(c * 1024 + zz * T + start_row, size), size)
+        dst = pl.ds(pl.multiple_of(zz * T + start_row, size), size)
+        return wg[p, src, cols] + ccr[p, dst, cols].astype(F32)
 
     def z_own(i):
-        for n in range(2):
+        for n in OWN:
             z_any(n, i)
 
     def z_other(i):
-        for n in range(2, 4):
+        for n in PAIR:
             z_any(n, i)
 
     def z_any(n, i):
@@ -286,49 +292,49 @@
             z_last(n)
             send_fin(n)
 
-    def on_core(h, work, *args):
+    def reducer(h, work, *args):
         @pl.when(c == h)
         def _():
             work(*args)
 
     def z_step(n, i):
+        p, first, width = CHUNKS[n]
+        cols = pl.ds(first, width)
         if i == 0:
             far = lax.rem(z + 4, 8)
-            zs[n, 0, steps[0], :] = pair_sum(n, far, 0, 64).astype(BF16)
-            zs[n, 1, steps[0], :] = pair_sum(n, far, 64, 64).astype(BF16)
-        else:
             for d in range(2):
-                zz = lax.rem(z + 4 - i, 8) if d == 0 else lax.rem(z + 4 + i, 8)
-                zc[n, d, i - 1].wait_recv()
-                if i == 1:
-                    for half in range(2):
-                        part = pair_sum(n, zz, half * 64, 64)
-                        if half == d:
-                            part = part + zr[n, d, steps[0], :].astype(F32)
-                        zs[n, d, pl.ds(64 + half * 64, 64), :] = part.astype(BF16)
-                else:
-                    part = pair_sum(n, zz) + zr[n, d, steps[i - 1], :].astype(F32)
-                    zs[n, d, steps[i], :] = part.astype(BF16)
-                start(zc[n, d, i])
-        if i == 0:
-            for d in range(2):
+                zs[p, d, steps[0], cols] = pair_sum(n, far, d * 64, 64).astype(BF16)
                 start(zc[n, d, 0])
+        for d in range(2) if i else ():
+            zz = lax.rem(z + 4 - i, 8) if d == 0 else lax.rem(z + 4 + i, 8)
+            zc[n, d, i - 1].wait_recv()
+            came = zr[p, d, steps[i - 1], cols].astype(F32)
+            if i == 1:
+                for half in range(2):
+                    part = pair_sum(n, zz, half * 64, 64)
+                    if half == d:
+                        part = part + came
+                    zs[p, d, pl.ds(64 + half * 64, 64), cols] = part.astype(BF16)
+            else:
+                zs[p, d, steps[i], cols] = (pair_sum(n, zz) + came).astype(BF16)
+            start(zc[n, d, i])
 
     def z_last(n):
+        p, first, width = CHUNKS[n]
+        cols = pl.ds(first, width)
         for d in range(2):
             zc[n, d, 3].wait_recv()
-        total = pair_sum(n, z) + zr[n, 0, steps[3], :].astype(F32) + zr[n, 1, steps[3], :].astype(F32)
-        fin[n] = total.astype(BF16)
+        came = zr[p, 0, steps[3], cols].astype(F32) + zr[p, 1, steps[3], cols].astype(F32)
+        fin[p, :, cols] = (pair_sum(n, z) + came).astype(BF16)
 
     left, right = pl.ds(0, HH), pl.ds(HH, HH)
 
-    def x_far():
-        for s in (1, 0):
-            block = pl.ds(3 * 256 + s * T, T)
-            xs[0, 0, s] = hg[block, left].astype(BF16)
-            start(xc[0, 0, s])
-            xs[1, 0, s] = hg[block, right].astype(BF16)
-            start(xc[1, 0, s])
+    def x_far(s):
+        block = pl.ds(3 * 256 + s * T, T)
+        xs[0, 0, s] = hg[block, left].astype(BF16)
+        start(xc[0, 0, s])
+        xs[1, 0, s] = hg[block, right].astype(BF16)
+        start(xc[1, 0, s])
 
     def x_direct(s):
         xs[0, 1, s] = hg[pl.ds(1 * 256 + s * T, T), right].astype(BF16)
@@ -353,25 +359,26 @@
         hi = hg[block, right] + xr[0, 1, s].astype(F32) + xr[1, 2, s].astype(F32)
         return lo.astype(BF16), hi.astype(BF16)
 
+    last, stay = [], []
+    for n, (p, first, width) in enumerate(CHUNKS):
+        cols = pl.ds(first, width)
+        target = dev(yhh=yl, yll=1 - yl) if p else dev(yhh=yl)
+        src, dst = fin.at[p, :, cols], yr.at[yh, :, cols]
+        last.append(remote(src, dst, target, yssem.at[n], yrsem.at[yh, n]))
+        stay.append(pltpu.make_async_copy(src, dst, yrsem.at[yh, n]))
+
     def send_fin(n):
-        if n < 2:
-
-            @pl.when(yh != yl)
-            def _():
-                last[n].start()
-        else:
+        if CHUNKS[n][0] == 1:
             last[n].start()
-
-    last = [
-        remote(
-            fin.at[n],
-            yr.at[yh, n % 2],
-            dev(yhh=yl) if n < 2 else dev(yhh=yl, yll=1 - yl),
-            yssem.at[n],
-            yrsem.at[yh, n % 2],
-        )
-        for n in range(4)
-    ]
+            return
+
+        @pl.when(yh != yl)
+        def _():
+            last[n].start()
+
+        @pl.when(yh == yl)
+        def _():
+            stay[n].start()
 
     def hid_in(h, r):
         if r == 3:
@@ -401,150 +408,165 @@
         g_y[r, 0].wait_recv()
         g_y[r, 1].wait_recv()
 
+    def w_in(k):
+        w_y[k].wait_recv()
+        start(w_z[k])
+        start(w_c[k])
+
+    def w_near(k):
+        w_z[k].wait_recv()
+        start(w_d[k])
+        turn(c, 1 - e, k)
+
+    def w_core(k):
+        w_c[k].wait_recv()
+        turn(1 - c, e, k)
+
+    def w_core_near(k):
+        w_d[k].wait_recv()
+        turn(1 - c, 1 - e, k)
+
     hg_own()
+    w_in(0)
     forward(0, 0)
     send_b(0)
     flip(0, 0)
     wg_add(0, 0, 0, 256, True)
-    w_y[0].wait_recv()
-    start(w_z[0])
-    start(w_c[0])
+    w_in(1)
+    turn(c, e, 0)
+    turn(c, e, 1)
     forward(0, 1)
     for i in range(2):
         start(a_p[1][i])
         start(a_m[1][1 - i])
-    turn(c, e, 0)
+    w_in(2)
+    w_near(0)
+    w_core(0)
+    turn(c, e, 2)
     hid_in(0, 1)
     hid_in(0, 2)
     flip(0, 1)
     flip(0, 2)
     wg_add(0, 0, 256, 512, False)
-    w_y[1].wait_recv()
-    start(w_z[1])
-    start(w_c[1])
-    w_c[0].wait_recv()
-    turn(1 - c, e, 0)
+    w_in(3)
+    w_near(1)
     hid_in(0, 3)
     flip(0, 3)
     wg_add(0, 0, 768, 256, False)
-    cc_send(0, 0)
-    cc_send(1, 0)
-    w_z[0].wait_recv()
-    start(w_d[0])
+    cc_send(OWN, 0)
+    turn(c, e, 3)
+    w_core(1)
     forward(1, 0)
     send_b(1)
-    on_core(0, z_own, 0)
-    turn(c, e, 1)
-    turn(c, 1 - e, 0)
+    w_near(2)
+    reducer(0, z_own, 0)
     flip(1, 0)
     wg_add(0, 1, 0, 256, True)
-    w_c[1].wait_recv()
-    turn(1 - c, e, 1)
-    w_d[0].wait_recv()
-    turn(1 - c, 1 - e, 0)
-    w_z[1].wait_recv()
-    start(w_d[1])
-    turn(c, 1 - e, 1)
     g_in(3)
-    w_d[1].wait_recv()
-    turn(1 - c, 1 - e, 1)
-    on_core(0, z_own, 1)
+    wg_add(1, 0, 768, 256, True)
+    w_core(2)
+    w_core(3)
+    w_core_near(0)
+    w_core_near(1)
+    w_near(3)
+    w_core_near(2)
+    reducer(0, z_own, 1)
+    w_core_near(3)
     hg_other(3)
     forward(1, 1)
-    x_far()
+    x_far(1)
+    g_in(1)
+    hg_other(1)
+    reducer(0, z_own, 2)
     hid_in(1, 1)
     hid_in(1, 2)
-    on_core(0, z_own, 2)
     flip(1, 1)
     flip(1, 2)
     wg_add(0, 1, 256, 512, False)
+    g_y[2, 0].wait_recv()
+    hg_other(2, 1)
+    x_direct(1)
     hid_in(1, 3)
     flip(1, 3)
     wg_add(0, 1, 768, 256, False)
-    cc_send(0, 1)
-    cc_send(1, 1)
-    g_in(1)
-    hg_other(1)
-    g_in(2)
-    hg_other(2)
-    x_direct(1)
-    on_core(1, z_own, 0)
-    wg_add(1, 0, 256, 768, True)
-    on_core(0, z_own, 3)
+    cc_send(OWN, 1)
+    reducer(0, z_own, 3)
+    g_y[2, 1].wait_recv()
+    hg_other(2, 0)
+    wg_add(1, 0, 256, 512, False)
     x_summed(1)
+    x_far(0)
     x_direct(0)
-    on_core(1, z_own, 1)
     wg_add(1, 1, 256, 768, True)
+    reducer(1, z_own, 0)
+    reducer(0, z_own, 4)
     g_in(0)
     for h in range(2):
         wg_add(1, h, 0, 256, False)
-        cc_send(2, h)
-        cc_send(3, h)
-    on_core(0, z_own, 4)
-    on_core(1, z_own, 2)
-    x_summed(0)
+        cc_send(PAIR, h)
+    reducer(1, z_own, 1)
+    hg_other(0)
     z_other(0)
-    hg_other(0)
-    on_core(1, z_own, 3)
+    reducer(1, z_own, 2)
     z_other(1)
-    on_core(1, z_own, 4)
     lo, hi = x_total(1)
     yos[:, left] = lo
     yos[:, right] = hi
     start(o_y)
+    reducer(1, z_own, 3)
     z_other(2)
+    x_summed(0)
+    reducer(1, z_own, 4)
     z_other(3)
-    z_any(2, 4)
+    z_other(4)
     lo, hi = x_total(0)
     os[:, left] = lo
     os[:, right] = hi
     put_mine = local(os, out_ref.at[:, mine], 5)
-    z_any(3, 4)
     o_y.wait_recv()
-    put_other = local(yor, out_ref.at[:, other], 6)
-
-    def arrived(slot, n):
-        pltpu.make_async_copy(yr.at[slot, n], yr.at[slot, n], yrsem.at[slot, n]).wait()
-
-    for n in range(2):
-        chunk = pl.ds(n * CW, CW)
-
-        @pl.when(yh == yl)
-        def _():
-            arrived(1 - yh, n)
-            gs[:, chunk] = fin[n].astype(F32) + yr[1 - yh, n].astype(F32)
-
-        @pl.when(yh != yl)
-        def _():
-            arrived(0, n)
-            arrived(1, n)
-            gs[:, chunk] = yr[0, n].astype(F32) + yr[1, n].astype(F32)
-
-    puts = [
-        local(gs.at[:, pl.ds(0, CQ)], gq_ref, 7),
-        local(gs.at[:, pl.ds(CQ, CK)], gk_ref, 8),
-        local(gs.at[:, pl.ds(CQ + CK, CK)], gv_ref, 9),
-    ]
+
+    def arrived(slot, chunks):
+        for n in chunks:
+            _, first, width = CHUNKS[n]
+            part = yr.at[slot, :, pl.ds(first, width)]
+            pltpu.make_async_copy(part, part, yrsem.at[slot, n]).wait()
+
+    @pl.when(yh == yl)
+    def _():
+        arrived(0, OWN)
+        arrived(1, OWN)
 
     @pl.when(yh != yl)
     def _():
-        last[0].wait_send()
-        last[1].wait_send()
-
-    last[2].wait_send()
-    last[3].wait_send()
+        arrived(0, PAIR)
+        arrived(1, PAIR)
+        for n in OWN:
+            last[n].wait_send()
+
+    for n in PAIR:
+        last[n].wait_send()
     for copy in sent:
         copy.wait_send()
-    for put in [put_mine, put_other] + puts:
-        put.wait()
-
-
-def hand_over(*refs):
-    sources, targets, through, (into, out) = refs[:4], refs[4:8], refs[8:12], refs[12:]
-    loads = [pltpu.make_async_copy(sources[i], through[i], into.at[i]) for i in range(4)]
-    stores = [pltpu.make_async_copy(through[i], targets[i], out.at[i]) for i in range(4)]
+    put_mine.wait()
+
+
+def hand_over(
+    out_ref, yr_ref, out, gq, gk, gv, out_buf, yr_buf, g_buf, into, away
+):
+    yr_load = pltpu.make_async_copy(yr_ref, yr_buf, into.at[4])
+    yr_load.start()
+    loads, stores = [], []
+    for i in range(4):
+        part = pl.ds(i * 32, 32)
+        loads.append(pltpu.make_async_copy(out_ref.at[part], out_buf.at[part], into.at[i]))
+        stores.append(pltpu.make_async_copy(out_buf.at[part], out.at[part], away.at[i]))
     for load in loads:
         load.start()
+    yr_load.wait()
+    g_buf[...] = yr_buf[0].astype(F32) + yr_buf[1].astype(F32)
+    for i, (ref, first, width) in enumerate(((gq, 0, CQ), (gk, CQ, CK), (gv, CQ + CK, CK))):
+        stores.append(pltpu.make_async_copy(g_buf.at[:, pl.ds(first, width)], ref, away.at[4 + i]))
+        stores[-1].start()
     for load, store in zip(loads, stores):
         load.wait()
         store.start()
@@ -552,7 +574,7 @@
         store.wait()
 
 
-N_SEM = 96
+N_SEM = 112
 
 
 def local_step(*args):
@@ -566,33 +588,31 @@
         pltpu.VMEM((C, H), BF16),
         pltpu.VMEM((512, C), BF16),
         pltpu.VMEM((1024, H), F32),
-        pltpu.VMEM((4, H, CW), F32),
-        pltpu.VMEM((4, 1024, CW), BF16),
-        pltpu.VMEM((4, 1024, CW), BF16),
+        pltpu.VMEM((2, H, C), F32),
+        pltpu.VMEM((2, 1024, C), BF16),
+        pltpu.VMEM((2, 1024, C), BF16),
         pltpu.VMEM((2, 3, 2, T, HH), BF16),
         pltpu.VMEM((2, 3, 2, T, HH), BF16),
-        pltpu.VMEM((4, 2, 448, CW), BF16),
-        pltpu.VMEM((4, 2, 448, CW), BF16),
-        pltpu.VMEM((4, T, CW), BF16),
-        pltpu.VMEM((2, 2, T, CW), BF16),
+        pltpu.VMEM((2, 2, 448, C), BF16),
+        pltpu.VMEM((2, 2, 448, C), BF16),
+        pltpu.VMEM((2, T, C), BF16),
         pltpu.VMEM((T, H), BF16),
         pltpu.VMEM((T, H), BF16),
-        pltpu.VMEM((T, H), BF16),
-        pltpu.VMEM((T, C), F32),
         pltpu.SemaphoreType.DMA((11,)),
         pltpu.SemaphoreType.DMA((N_SEM,)),
         pltpu.SemaphoreType.DMA((N_SEM,)),
-        pltpu.SemaphoreType.DMA((4,)),
-        pltpu.SemaphoreType.DMA((2, 2)),
+        pltpu.SemaphoreType.DMA((len(CHUNKS),)),
+        pltpu.SemaphoreType.DMA((2, len(CHUNKS))),
     ]
     anywhere = pl.BlockSpec(memory_space=pl.ANY)
     shapes = [((T, D), BF16), ((T, CQ), F32), ((T, CK), F32), ((T, CK), F32)]
     out_shape = tuple(jax.ShapeDtypeStruct(*shape) for shape in shapes)
+    terms = jax.ShapeDtypeStruct((2, T, C), BF16)
     results = pl.pallas_call(
         kernel,
-        out_shape=out_shape,
+        out_shape=(out_shape[0], terms),
         in_specs=[anywhere] * 7,
-        out_specs=(anywhere,) * 4,
+        out_specs=(anywhere, anywhere),
         scratch_shapes=scratch,
         compiler_params=pltpu.CompilerParams(
             collective_id=0, has_side_effects=True, vmem_limit_bytes=67043328
@@ -601,10 +621,15 @@
     return pl.pallas_call(
         hand_over,
         out_shape=out_shape,
-        in_specs=[anywhere] * 4,
+        in_specs=[anywhere] * 2,
         out_specs=(anywhere,) * 4,
-        scratch_shapes=[pltpu.VMEM(*shape) for shape in shapes]
-        + [pltpu.SemaphoreType.DMA((4,)), pltpu.SemaphoreType.DMA((4,))],
+        scratch_shapes=[
+            pltpu.VMEM((T, D), BF16),
+            pltpu.VMEM((2, T, C), BF16),
+            pltpu.VMEM((T, C), F32),
+            pltpu.SemaphoreType.DMA((5,)),
+            pltpu.SemaphoreType.DMA((7,)),
+        ],
         cost_estimate=pl.CostEstimate(flops=0, bytes_accessed=3 << 20, transcendentals=0),
     )(*results)
 

time: 90 us -> 88 us (0.978)
  Pallas kernels: 88.4 us -> 87.3 us
    pallas_call x2, Pallas kernels: 88.4 us -> 87.3 us  [the longest x1 85 us: local_step(): pl.pallas_call(kernel, out_shape=(out_shape[0], terms), in_specs=[anywher...]
where the time goes in v4:
time: 88 us; the launch traced here: 87.9 us
  Pallas kernels  87.3 us (99%)
    pallas_call x1, Pallas kernels, local_step(): pl.pallas_call(kernel, out_shape=(out_shape[0], terms), in_specs=[anywher...  85 us
    pallas_call x1, Pallas kernels, local_step(): pl.pallas_call(hand_over, out_shape=out_shape, in_specs=[anywhere] * 2, o...  2.24 us

profile of v4, /device:TPU:9, one launch (start us, length us, event | category | flops | bytes accessed | tf_op | source)
XLA Modules:
  0.0 87.9 jit_solution(6485698947913995497)
XLA Ops:
  0.6 85.0 %shard_map.102 = (bf16[128,4096]{1,0:T(8,128)(2,1)}, bf16[2,128,768]{2,1,0:T(8,128)(2,1)}) custom-call(bf16[128,4096]{1,0:T(8,128)(2,1)} %hidden_ref.1, bf16[1024,512]{1,0:T(8,128)(2,1)} %q_ref.1, bf16[1024,128]{1,0:T(8,128)(2,1)} %k_ref.1, bf16[1024,128]{1,0:T(8,128)(2,1)} %v_ref.1, bf16[4096,512]{1,0:T(8,128)(2,1)} %wq_ref.1, bf16[4096,128]{1,0:T(8,128)(2,1)} %wk_ref.1, ...), custom_call_target="tpu_custom_call" | custom-call | tf_op jit(solution)/shard_map/pallas_call | solution.py:611
  85.7 2.2 %shard_map.103 = (bf16[128,4096]{1,0:T(8,128)(2,1)}, f32[128,512]{1,0:T(8,128)}, f32[128,128]{1,0:T(8,128)}, f32[128,128]{1,0:T(8,128)}) custom-call(bf16[128,4096]{1,0:T(8,128)(2,1)} %get-tuple-element.6.out_ref, bf16[2,128,768]{2,1,0:T(8,128)(2,1)} %get-tuple-element.7.yr_ref), custom_call_target="tpu_custom_call" | custom-call | bytes 3145728 | tf_op jit(solution)/shard_map/pallas_call | solution.py:621

commit v5 on v4

--- a/solution.py
+++ b/solution.py
@@ -15,9 +15,10 @@
 CQ = 512
 CK = 128
 C = 768
-CHUNKS = ((0, 0, 384), (0, 384, 384), (1, 0, 256), (1, 256, 256), (1, 512, 256))
+CHUNKS = ((0, 0, 384), (0, 384, 384), (1, 0, 256), (1, 256, 256), (1, 512, 128), (1, 640, 128))
 OWN = (0, 1)
-PAIR = (2, 3, 4)
+POS = {(0, 0): 0, (0, 1): 1, (1, 0): 2, (2, 0): 3, (1, 1): 4, (2, 1): 5, (3, 0): 6, (3, 1): 7}
+PAIR = (2, 3, 4, 5)
 
 
 def nt(left, right):
@@ -108,6 +109,10 @@
         if not any(copy is one for one in sent):
             sent.append(copy)
 
+    barrier = pltpu.get_barrier_semaphore()
+    for target in (XP, XM, YI, YO, Y2, ZP, ZM, CC):
+        pl.semaphore_signal(barrier, inc=1, device_id=target, device_id_type=MESH)
+
     def local(src, dst, i):
         copy = pltpu.make_async_copy(src, dst, lsem.at[i])
         copy.start()
@@ -132,7 +137,7 @@
         for s in range(2):
             block = lax.rem(x + off, 4) * 2 + (yl if s == 0 else 1 - yl)
             src = pl.ds(pl.multiple_of(block * T, T), T)
-            dst = pl.ds(r * 256 + s * T, T)
+            dst = pl.ds(POS[r, s] * T, T)
             local(q_ref.at[src], gown.at[dst, pl.ds(0, CQ)], 3)
             local(k_ref.at[src], gown.at[dst, pl.ds(CQ, CK)], 3)
             local(v_ref.at[src], gown.at[dst, pl.ds(CQ + CK, CK)], 3)
@@ -143,13 +148,10 @@
     def wait_local(buffer, i):
         pltpu.make_async_copy(buffer, buffer, lsem.at[i]).wait()
 
-    barrier = pltpu.get_barrier_semaphore()
-    for target in (XP, XM, YI, YO, Y2, ZP, ZM, CC):
-        pl.semaphore_signal(barrier, inc=1, device_id=target, device_id_type=MESH)
     pl.semaphore_wait(barrier, 8)
 
     def rows(r, s, half=None):
-        first = r * 256 + s * T
+        first = POS[r, s] * T
         return pl.ds(first, T) if half is None else pl.ds(first + half * 64, 64)
 
     def piece(h, r, s, i):
@@ -204,11 +206,14 @@
     for k in range(4):
         start(w_y[k])
     wait_local(gown, 3)
-    for r in (3, 1, 2, 0):
-        for s in (0, 1):
-            start(g_y[r, s])
-        if r == 3:
-            start(b_y[1])
+    start(g_y[3, 0])
+    start(g_y[3, 1])
+    start(b_y[1])
+    for s in range(2):
+        start(g_y[1, s])
+        start(g_y[2, s])
+    start(g_y[0, 0])
+    start(g_y[0, 1])
     wait_local(hid.at[1, :, pl.ds(0, T)], 10)
     wait_local(wh.at[:, pl.ds(0, C)], 4)
 
@@ -226,8 +231,8 @@
         piece = wpiece(cc, ee, k)
         wt[:, piece] = woth[piece, :].T
 
-    def hg_other(r, s=None):
-        block = pl.ds(r * 256, 256) if s is None else pl.ds(r * 256 + s * T, T)
+    def hg_other(group):
+        block = pl.ds(group * 256, 256)
 
         def step(n, carry):
             cols = pl.ds(pl.multiple_of(n * 512, 512), 512)
@@ -337,17 +342,17 @@
         start(xc[1, 0, s])
 
     def x_direct(s):
-        xs[0, 1, s] = hg[pl.ds(1 * 256 + s * T, T), right].astype(BF16)
+        xs[0, 1, s] = hg[rows(1, s), right].astype(BF16)
         start(xc[0, 1, s])
-        xs[1, 1, s] = hg[pl.ds(2 * 256 + s * T, T), left].astype(BF16)
+        xs[1, 1, s] = hg[rows(2, s), left].astype(BF16)
         start(xc[1, 1, s])
 
     def x_summed(s):
         xc[0, 0, s].wait_recv()
-        xs[0, 2, s] = (hg[pl.ds(1 * 256 + s * T, T), left] + xr[0, 0, s].astype(F32)).astype(BF16)
+        xs[0, 2, s] = (hg[rows(1, s), left] + xr[0, 0, s].astype(F32)).astype(BF16)
         start(xc[0, 2, s])
         xc[1, 0, s].wait_recv()
-        xs[1, 2, s] = (hg[pl.ds(2 * 256 + s * T, T), right] + xr[1, 0, s].astype(F32)).astype(BF16)
+        xs[1, 2, s] = (hg[rows(2, s), right] + xr[1, 0, s].astype(F32)).astype(BF16)
         start(xc[1, 2, s])
 
     def x_total(s):
@@ -380,16 +385,17 @@
         def _():
             stay[n].start()
 
-    def hid_in(h, r):
-        if r == 3:
+    def hid_in(h, group):
+        if group == 3:
             for s in range(2):
                 f_p[h][s].wait_recv()
                 f_m[h][s].wait_recv()
+        elif group == 1:
+            a_p[h][1].wait_recv()
+            a_m[h][0].wait_recv()
         else:
-            copies = (a_p[h], b_p[h]) if r == 2 else (a_m[h], b_m[h])
-            i = 1 if r == 2 else 0
-            for copy in copies:
-                copy[i].wait_recv()
+            b_p[h][1].wait_recv()
+            b_m[h][0].wait_recv()
 
     def forward(h, s):
         src_p, src_m = (b_p, b_m) if s else (a_p, a_m)
@@ -404,9 +410,10 @@
             start(b_p[h][i])
             start(b_m[h][1 - i])
 
-    def g_in(r):
-        g_y[r, 0].wait_recv()
-        g_y[r, 1].wait_recv()
+    def g_in(group):
+        pairs = ((0, 0), (0, 1)), ((1, 1), (2, 1)), ((1, 0), (2, 0)), ((3, 0), (3, 1))
+        for pair in pairs[group]:
+            g_y[pair].wait_recv()
 
     def w_in(k):
         w_y[k].wait_recv()
@@ -427,14 +434,16 @@
         turn(1 - c, 1 - e, k)
 
     hg_own()
-    w_in(0)
     forward(0, 0)
     send_b(0)
+    w_in(0)
     flip(0, 0)
     wg_add(0, 0, 0, 256, True)
     w_in(1)
     turn(c, e, 0)
     turn(c, e, 1)
+    hid_in(0, 1)
+    flip(0, 1)
     forward(0, 1)
     for i in range(2):
         start(a_p[1][i])
@@ -443,9 +452,7 @@
     w_near(0)
     w_core(0)
     turn(c, e, 2)
-    hid_in(0, 1)
     hid_in(0, 2)
-    flip(0, 1)
     flip(0, 2)
     wg_add(0, 0, 256, 512, False)
     w_in(3)
@@ -473,26 +480,25 @@
     reducer(0, z_own, 1)
     w_core_near(3)
     hg_other(3)
+    hid_in(1, 1)
+    flip(1, 1)
+    wg_add(0, 1, 256, 256, False)
     forward(1, 1)
     x_far(1)
-    g_in(1)
-    hg_other(1)
+    g_in(2)
+    hg_other(2)
+    x_direct(1)
     reducer(0, z_own, 2)
-    hid_in(1, 1)
     hid_in(1, 2)
-    flip(1, 1)
     flip(1, 2)
-    wg_add(0, 1, 256, 512, False)
-    g_y[2, 0].wait_recv()
-    hg_other(2, 1)
-    x_direct(1)
+    wg_add(0, 1, 512, 256, False)
     hid_in(1, 3)
     flip(1, 3)
     wg_add(0, 1, 768, 256, False)
     cc_send(OWN, 1)
     reducer(0, z_own, 3)
-    g_y[2, 1].wait_recv()
-    hg_other(2, 0)
+    g_in(1)
+    hg_other(1)
     wg_add(1, 0, 256, 512, False)
     x_summed(1)
     x_far(0)
@@ -574,7 +580,7 @@
         store.wait()
 
 
-N_SEM = 112
+N_SEM = 120
 
 
 def local_step(*args):

time: 88 us -> 88.1 us (level)
  no operation moved by 1% of the time
where the time goes in v5:
time: 88.1 us; the launch traced here: 88 us
  Pallas kernels  87.4 us (99%)
    pallas_call x1, Pallas kernels, local_step(): pl.pallas_call(kernel, out_shape=(out_shape[0], terms), in_specs=[anywher...  85.1 us
    pallas_call x1, Pallas kernels, local_step(): pl.pallas_call(hand_over, out_shape=out_shape, in_specs=[anywhere] * 2, o...  2.24 us

profile of v5, /device:TPU:9, one launch (start us, length us, event | category | flops | bytes accessed | tf_op | source)
XLA Modules:
  0.0 88.0 jit_solution(11234448179393839813)
XLA Ops:
  0.6 85.1 %shard_map.102 = (bf16[128,4096]{1,0:T(8,128)(2,1)}, bf16[2,128,768]{2,1,0:T(8,128)(2,1)}) custom-call(bf16[128,4096]{1,0:T(8,128)(2,1)} %hidden_ref.1, bf16[1024,512]{1,0:T(8,128)(2,1)} %q_ref.1, bf16[1024,128]{1,0:T(8,128)(2,1)} %k_ref.1, bf16[1024,128]{1,0:T(8,128)(2,1)} %v_ref.1, bf16[4096,512]{1,0:T(8,128)(2,1)} %wq_ref.1, bf16[4096,128]{1,0:T(8,128)(2,1)} %wk_ref.1, ...), custom_call_target="tpu_custom_call" | custom-call | tf_op jit(solution)/shard_map/pallas_call | solution.py:617
  85.8 2.2 %shard_map.103 = (bf16[128,4096]{1,0:T(8,128)(2,1)}, f32[128,512]{1,0:T(8,128)}, f32[128,128]{1,0:T(8,128)}, f32[128,128]{1,0:T(8,128)}) custom-call(bf16[128,4096]{1,0:T(8,128)(2,1)} %get-tuple-element.6.out_ref, bf16[2,128,768]{2,1,0:T(8,128)(2,1)} %get-tuple-element.7.yr_ref), custom_call_target="tpu_custom_call" | custom-call | bytes 3145728 | tf_op jit(solution)/shard_map/pallas_call | solution.py:627

commit v6 on v4

--- a/solution.py
+++ b/solution.py
@@ -427,9 +427,9 @@
         turn(1 - c, 1 - e, k)
 
     hg_own()
-    w_in(0)
     forward(0, 0)
     send_b(0)
+    w_in(0)
     flip(0, 0)
     wg_add(0, 0, 0, 256, True)
     w_in(1)

time: 88 us -> 88 us (level)
  no operation moved by 1% of the time
where the time goes in v6:
time: 88 us; the launch traced here: 87.9 us
  Pallas kernels  87.3 us (99%)
    pallas_call x1, Pallas kernels, local_step(): pl.pallas_call(kernel, out_shape=(out_shape[0], terms), in_specs=[anywher...  85 us
    pallas_call x1, Pallas kernels, local_step(): pl.pallas_call(hand_over, out_shape=out_shape, in_specs=[anywhere] * 2, o...  2.24 us

profile of v6, /device:TPU:9, one launch (start us, length us, event | category | flops | bytes accessed | tf_op | source)
XLA Modules:
  0.0 87.9 jit_solution(3418363869412990527)
XLA Ops:
  0.6 85.0 %shard_map.102 = (bf16[128,4096]{1,0:T(8,128)(2,1)}, bf16[2,128,768]{2,1,0:T(8,128)(2,1)}) custom-call(bf16[128,4096]{1,0:T(8,128)(2,1)} %hidden_ref.1, bf16[1024,512]{1,0:T(8,128)(2,1)} %q_ref.1, bf16[1024,128]{1,0:T(8,128)(2,1)} %k_ref.1, bf16[1024,128]{1,0:T(8,128)(2,1)} %v_ref.1, bf16[4096,512]{1,0:T(8,128)(2,1)} %wq_ref.1, bf16[4096,128]{1,0:T(8,128)(2,1)} %wk_ref.1, ...), custom_call_target="tpu_custom_call" | custom-call | tf_op jit(solution)/shard_map/pallas_call | solution.py:611
  85.7 2.2 %shard_map.103 = (bf16[128,4096]{1,0:T(8,128)(2,1)}, f32[128,512]{1,0:T(8,128)}, f32[128,128]{1,0:T(8,128)}, f32[128,128]{1,0:T(8,128)}) custom-call(bf16[128,4096]{1,0:T(8,128)(2,1)} %get-tuple-element.6.out_ref, bf16[2,128,768]{2,1,0:T(8,128)(2,1)} %get-tuple-element.7.yr_ref), custom_call_target="tpu_custom_call" | custom-call | bytes 3145728 | tf_op jit(solution)/shard_map/pallas_call | solution.py:621
